TPU v7x, 8 devices: a whole 2x2x1 slice. The times are simulated.
8 devices in a mesh: model: 2 (over z, y), data: 4 (over x, core).
Axes of the slice: x: 2, y: 2, z: 1, core: 2. Of those that a mesh axis runs over, the one named last changes fastest.
Arguments:
- x_tokens: bfloat16 [16384, 2048], P('data')
- dy_tokens: bfloat16 [16384, 2048], P('data')
- w_col: bfloat16 [2, 2048, 2048], P(None, None, 'model')
- w_row: bfloat16 [2, 2048, 2048], P(None, 'model')
- a_old_col: float32 [2, 2048, 2048], replicated
- s_old_col: float32 [2, 2048, 1024], P(None, 'model')
- a_old_row: float32 [2, 2048, 1024], P(None, 'model')
- s_old_row: float32 [2, 2048, 2048], replicated
- a_inv_col: float32 [2, 2048, 2048], replicated
- s_inv_col: float32 [2, 2048, 1024], P(None, 'model')
- a_inv_row: float32 [2, 2048, 1024], P(None, 'model')
- s_inv_row: float32 [2, 2048, 2048], replicated
Outputs:
- output 1: float32 [2, 2048, 2048], P(None, None, 'model')
- output 2: float32 [2, 2048, 2048], P(None, 'model')
- output 3: float32 [2, 2048, 2048], replicated
- output 4: float32 [2, 2048, 1024], P(None, 'model')
- output 5: float32 [2, 2048, 1024], P(None, 'model')
- output 6: float32 [2, 2048, 2048], replicated
All inputs are finite; a program needn't handle non-finite values.
Results may differ from a plain program's by a relative error of at most 0.00457.
Values are sent between devices in bfloat16 or wider.
A program may use at most 1.25 GiB of HBM per device.

v0:
```python
import math
import jax
import jax.numpy as jnp
from jax import lax
from jax.sharding import PartitionSpec as P

FACTOR_DECAY = 0.8
GELU_SCALE = math.sqrt(2.0 / math.pi)
GELU_CUBIC = 0.044715
EXACT = lax.Precision.HIGHEST
TN_DIMS = (((0,), (0,)), ((), ()))
NT_DIMS = (((1,), (1,)), ((), ()))


def gelu_value(pre_act):
    tanh_arg = GELU_SCALE * (pre_act + GELU_CUBIC * pre_act * pre_act * pre_act)
    return 0.5 * pre_act * (1.0 + jnp.tanh(tanh_arg))


def gelu_slope(pre_act):
    tanh_arg = GELU_SCALE * (pre_act + GELU_CUBIC * pre_act * pre_act * pre_act)
    tanh_val = jnp.tanh(tanh_arg)
    return 0.5 * (1.0 + tanh_val) + 0.5 * pre_act * (1.0 - tanh_val * tanh_val) * GELU_SCALE * (1.0 + 3.0 * GELU_CUBIC * pre_act * pre_act)


def activate(pre_act):
    return gelu_value(pre_act.astype(jnp.float32)).astype(jnp.bfloat16)


def back_gate(grad_act, pre_act):
    return (grad_act.astype(jnp.float32) * gelu_slope(pre_act.astype(jnp.float32))).astype(jnp.bfloat16)


def matmul(left_mat, right_mat):
    return jnp.dot(left_mat, right_mat, preferred_element_type=jnp.float32)


def matmul_tn(left_mat, right_mat):
    return lax.dot_general(left_mat, right_mat, TN_DIMS, preferred_element_type=jnp.float32)


def matmul_nt(left_mat, right_mat):
    return lax.dot_general(left_mat, right_mat, NT_DIMS, preferred_element_type=jnp.float32)


def exact_dot(left_mat, right_mat):
    return jnp.dot(left_mat, right_mat, precision=EXACT, preferred_element_type=jnp.float32)


def precondition(a_inv, grad_mat, s_inv):
    return exact_dot(exact_dot(a_inv, grad_mat), s_inv)


def blend_factor(old_mats, first_new, second_new, inv_rows):
    return FACTOR_DECAY * old_mats + (1.0 - FACTOR_DECAY) * inv_rows * jnp.stack([first_new, second_new])


def local_pass(x_tokens, dy_tokens, w_col, w_row):
    z_one = matmul(x_tokens, w_col[0]).astype(jnp.bfloat16)
    h_one = activate(z_one)
    z_two = lax.psum(matmul(h_one, w_row[0]), 'model').astype(jnp.bfloat16)
    h_two = activate(z_two)
    z_three = matmul(h_two, w_col[1]).astype(jnp.bfloat16)
    h_three = activate(z_three)
    g_three = back_gate(matmul_nt(dy_tokens, w_row[1]).astype(jnp.bfloat16), z_three)
    dh_two = lax.psum(matmul_nt(g_three, w_col[1]), 'model').astype(jnp.bfloat16)
    g_two = back_gate(dh_two, z_two)
    g_one = back_gate(matmul_nt(g_two, w_row[0]).astype(jnp.bfloat16), z_one)
    return [x_tokens, h_one, h_two, h_three], [g_one, g_two, g_three, dy_tokens]


def finish_step(totals, inv_rows, a_old_col, s_old_col, a_old_row, s_old_row, a_inv_col, s_inv_col, a_inv_row, s_inv_row):
    weight_grads = [total_mat * inv_rows for total_mat in totals[8:]]
    u_col = jnp.stack([precondition(a_inv_col[0], weight_grads[0], s_inv_col[0]), precondition(a_inv_col[1], weight_grads[2], s_inv_col[1])])
    u_row = jnp.stack([precondition(a_inv_row[0], weight_grads[1], s_inv_row[0]), precondition(a_inv_row[1], weight_grads[3], s_inv_row[1])])
    a_new_col = blend_factor(a_old_col, totals[0], totals[2], inv_rows)
    s_new_col = blend_factor(s_old_col, totals[4], totals[6], inv_rows)
    a_new_row = blend_factor(a_old_row, totals[1], totals[3], inv_rows)
    s_new_row = blend_factor(s_old_row, totals[5], totals[7], inv_rows)
    return (u_col, u_row, a_new_col, s_new_col, a_new_row, s_new_row)


def solution(mesh):
    data_ways = mesh.shape['data']

    def shard_body(x_tokens, dy_tokens, w_col, w_row, a_old_col, s_old_col, a_old_row, s_old_row, a_inv_col, s_inv_col, a_inv_row, s_inv_row):
        layer_in, layer_grad = local_pass(x_tokens, dy_tokens, w_col, w_row)
        local_sums = [matmul_tn(layer_in[layer], layer_in[layer]) for layer in range(4)]
        local_sums += [matmul_tn(layer_grad[layer], layer_grad[layer]) for layer in range(4)]
        local_sums += [matmul_tn(layer_in[layer], layer_grad[layer]) for layer in range(4)]
        totals = lax.psum(local_sums, 'data')
        inv_rows = 1.0 / (x_tokens.shape[0] * data_ways)
        return finish_step(totals, inv_rows, a_old_col, s_old_col, a_old_row, s_old_row, a_inv_col, s_inv_col, a_inv_row, s_inv_row)

    batch_split = P('data', None)
    col_split = P(None, None, 'model')
    row_split = P(None, 'model', None)
    replicated = P()
    return jax.shard_map(
        shard_body,
        mesh=mesh,
        in_specs=(batch_split, batch_split, col_split, row_split, replicated, row_split, row_split, replicated, replicated, row_split, row_split, replicated),
        out_specs=(col_split, row_split, replicated, row_split, row_split, replicated),
        check_vma=False,
    )
```

profile of v0, /device:TPU:0, one launch (start us, length us, event | category | flops | bytes accessed | tf_op | source)
XLA Modules:
  0.0 4505.7 jit_solution(5775508335637719292)
XLA Ops:
  7.2 0.0 all-reduce.5.cloned.1.call-start
  7.2 0.0 copy-start.4
  7.2 43.8 convolution_bitcast_fusion.3
  51.0 0.0 copy-done.4
  51.0 20.6 convolution_convert_fusion.1
  71.6 0.0 copy-start.6
  71.6 3.4 copy-done.6
  75.0 17.5 convolution_bitcast_fusion.8
  92.5 0.0 slice-start.5
  92.5 43.8 convolution_bitcast_fusion
  136.3 0.0 slice-done.4
  136.3 0.0 slice-done.5
  136.3 26.7 fusion.69
  163.0 760.9 %all-reduce.6 = bf16[4096,2048]{1,0:T(8,128)(2,1)} all-reduce(f32[4096,2048]{1,0:T(8,128)} %fusion.69), channel_id=1, replica_groups=mesh['model'=2,'data'=4] {'model'}, use_global_device_ids=true, to_apply=%region_0.0 | all-reduce | flops 8388608 | bytes 50331648 | tf_op jit(solution)/shard_map/psum | solution.py:61
  923.9 13.6 fusion.2
  937.5 0.0 copy-start
  937.5 6.2 copy-done
  943.7 21.6 convolution_convert_fusion
  965.3 0.0 copy-start.7
  965.3 23.8 convolution_bitcast_fusion.7
  989.1 0.0 copy-done.7
  989.1 32.7 fusion.21
  1021.8 32.0 fusion.92
  1053.8 15.4 convolution_bitcast_fusion.9
  1069.2 0.0 slice-done
  1069.2 0.0 slice-done.1
  1069.2 0.0 slice-done.2
  1069.2 0.0 slice-done.3
  1069.3 21.1 fusion.98
  1090.3 43.8 convolution_bitcast_fusion.2
  1134.1 25.5 fusion.65
  1159.6 753.9 %all-reduce.7 = bf16[4096,2048]{1,0:T(8,128)(2,1)} all-reduce(f32[4096,2048]{1,0:T(8,128)} %fusion.65), channel_id=1, replica_groups=mesh['model'=2,'data'=4] {'model'}, use_global_device_ids=true, to_apply=%region_1.0 | all-reduce | flops 8388608 | bytes 50331648 | tf_op jit(solution)/shard_map/psum | solution.py:66
  1913.5 27.1 fusion.7
  1940.6 31.9 fusion.28
  1972.5 31.5 fusion.95
  2004.0 44.0 convolution_bitcast_fusion.1
  2048.0 10.4 convolution_bitcast_fusion.10
  2058.4 21.8 convolution_bitcast_fusion.6
  2080.2 0.0 all-reduce.5.cloned.1.call-update
  2080.2 1900.2 %all-reduce.5.cloned.1.call-done = (f32[2048,1024]{0,1:T(8,128)}, f32[2048,1024]{0,1:T(8,128)}, f32[1024,2048]{1,0:T(8,128)}, f32[1024,2048]{1,0:T(8,128)}, f32[...) async-done(((f32[2048,1024]{0,1:T(8,128)}, ...) | async-done | bytes 117440528 | tf_op jit(solution)/shard_map/psum | solution.py:91
  3980.4 69.0 %fusion.39 = f32[1024,2048]{1,0:T(8,128)} fusion(f32[2,2048,2048]{2,1,0:T(8,128)} %param.20, f32[2048,1024]{0,1:T(8,128)} %get-tuple-element.6), kind=kOutput, calls=%fused_computation.64 | convolution fusion | flops 51541704704 | bytes 33554432 | tf_op jit(solution)/shard_map/dot_general | solution.py:47
  4049.4 0.0 copy-done.5
  4049.4 57.2 %fusion.41 = f32[1024,2048]{1,0:T(8,128)} fusion(f32[2,2048,2048]{2,1,0:T(8,128)} %param.20, f32[2048,1024]{0,1:T(8,128)S(1)} %copy-done.5), kind=kOutput, calls=%fused_computation.66 | convolution fusion | flops 51541704704 | bytes 33554432 | tf_op jit(solution)/shard_map/dot_general | solution.py:47
  4106.6 0.0 slice-done.6
  4106.6 0.0 slice-done.7
  4106.6 0.0 slice-start.8
  4106.6 31.6 convolution_bitcast_fusion.5
  4138.3 0.0 slice-start.9
  4138.3 30.1 convolution_bitcast_fusion.4
  4168.4 0.0 slice-done.8
  4168.4 0.0 slice-done.9
  4168.4 56.0 %fusion.49 = f32[2048,1024]{1,0:T(8,128)} fusion(f32[1024,2048]{1,0:T(8,128)} %get-tuple-element.8, f32[2,1024,1024]{2,1,0:T(8,128)S(1)} %bitcast.118), kind=kOutput, calls=%fused_computation.80 | convolution fusion | flops 25771900928 | bytes 20971520 | tf_op jit(solution)/shard_map/dot_general | solution.py:47
  4224.5 56.4 %fusion.51 = f32[2048,1024]{1,0:T(8,128)} fusion(f32[1024,2048]{1,0:T(8,128)} %get-tuple-element.9, f32[2,1024,1024]{2,1,0:T(8,128)S(1)} %bitcast.118), kind=kOutput, calls=%fused_computation.82 | convolution fusion | flops 25771900928 | bytes 20971520 | tf_op jit(solution)/shard_map/dot_general | solution.py:47
  4280.9 58.9 %fusion.55 = f32[1,1024,2048]{2,1,0:T(8,128)} fusion(f32[2048,1024]{1,0:T(8,128)} %fusion.51, f32[2,2048,2048]{2,1,0:T(8,128)} %param.23), kind=kOutput, calls=%fused_computation.88 | convolution fusion | flops 51539607552 | bytes 33554432 | tf_op jit(solution)/shard_map/dot_general | solution.py:47
  4339.8 59.2 %fusion.58 = f32[1,1024,2048]{2,1,0:T(8,128)} fusion(f32[2048,1024]{1,0:T(8,128)} %fusion.49, f32[2,2048,2048]{2,1,0:T(8,128)} %param.23), kind=kOutput, calls=%fused_computation.89 | convolution fusion | flops 51539607552 | bytes 33554432 | tf_op jit(solution)/shard_map/dot_general | solution.py:47
  4399.0 0.0 copy-start.1
  4399.0 0.0 copy-start.2
  4399.0 8.4 pad_maximum_fusion
  4407.5 0.0 copy-done.1
  4407.5 3.0 copy-done.2
  4410.5 6.6 pad_maximum_fusion.1
  4417.1 0.0 copy-done.3
  4417.1 16.4 fusion.47
  4433.5 64.8 %fusion.11 = (f32[2,2048,2048]{2,1,0:T(8,128)}, f32[2,2048,2048]{2,1,0:T(8,128)}) fusion(f32[1,2048,2048]{2,1,0:T(8,128)} %get-tuple-element.10, f32[1,2048,2048]{2,1,0:T(8,128)} %get-tuple-element.11, f32[2,2048,2048]{2,1,0:T(8,128)} %param.16, f32[1,2048,2048]{2,1,0:T(8,128)} %get-tuple-element.16, f32[1,2048,2048]{2,1,0:T(8,128)} %get-tuple-element.17, ...), kind=kLoop, calls=%fused_computation.33 | loop fusion | flops 67108864 | bytes 201326592 | tf_op jit(solution)/shard_map/add | solution.py:55
  (13 shorter events, 0.0 us)
Async XLA Ops:
  7.2 3973.2 %all-reduce.5.cloned.1.call-start = ((), (), s32[]{:S(2)}) async-start(), calls=%async_computation | async-start | bytes 234881024 | tf_op jit(solution)/shard_map/psum | solution.py:91
  7.2 43.8 copy-start.4
  71.6 3.4 copy-start.6
  75.0 61.3 %slice-start.4 = ((s8[8388608]{0:T(1024)(128)(4,1)}), s8[4194304]{0:T(1024)(128)(4,1)S(1)}, s32[]{:S(2)}) async-start(s8[8388608]{0:T(1024)(128)(4,1)} %bitcast.113), calls=%async_computation.5 | async-start | bytes 8388608
  92.5 43.8 slice-start.5
  937.5 6.2 copy-start
  965.3 23.8 copy-start.7
  1021.8 47.4 %slice-start = ((s8[16777216]{0:T(1024)(128)(4,1)}), s8[4194304]{0:T(1024)(128)(4,1)S(1)}, s32[]{:S(2)}) async-start(s8[16777216]{0:T(1024)(128)(4,1)} %bitcast.111), calls=%async_computation.1 | async-start | bytes 8388608
  1021.8 47.4 %slice-start.1 = ((s8[16777216]{0:T(1024)(128)(4,1)}), s8[4194304]{0:T(1024)(128)(4,1)S(1)}, s32[]{:S(2)}) async-start(s8[16777216]{0:T(1024)(128)(4,1)} %bitcast.111), calls=%async_computation.2 | async-start | bytes 8388608
  1021.8 47.4 %slice-start.2 = ((s8[16777216]{0:T(1024)(128)(4,1)}), s8[4194304]{0:T(1024)(128)(4,1)S(1)}, s32[]{:S(2)}) async-start(s8[16777216]{0:T(1024)(128)(4,1)} %bitcast.111), calls=%async_computation.3 | async-start | bytes 8388608
  1053.8 15.4 slice-start.3
  3980.4 69.0 %copy-start.5 = (f32[2048,1024]{0,1:T(8,128)S(1)}, f32[2048,1024]{0,1:T(8,128)}, u32[]{:S(2)}) copy-start(f32[2048,1024]{0,1:T(8,128)} %get-tuple-element.7) | copy-start | bytes 25165828
  3980.4 126.2 %slice-start.6 = ((s8[8388608]{0:T(1024)(128)(4,1)}), s8[4194304]{0:T(1024)(128)(4,1)S(1)}, s32[]{:S(2)}) async-start(s8[8388608]{0:T(1024)(128)(4,1)} %bitcast.115), calls=%async_computation.7 | async-start | bytes 8388608
  4049.4 57.2 %slice-start.7 = ((s8[8388608]{0:T(1024)(128)(4,1)}), s8[4194304]{0:T(1024)(128)(4,1)S(1)}, s32[]{:S(2)}) async-start(s8[8388608]{0:T(1024)(128)(4,1)} %bitcast.115), calls=%async_computation.8 | async-start | bytes 8388608
  4106.6 61.8 %slice-start.8 = ((s8[8388608]{0:T(1024)(128)(4,1)}), s8[4194304]{0:T(1024)(128)(4,1)S(1)}, s32[]{:S(2)}) async-start(s8[8388608]{0:T(1024)(128)(4,1)} %bitcast.117), calls=%async_computation.9 | async-start | bytes 8388608
  4138.3 30.1 slice-start.9
  4399.0 8.5 copy-start.1
  4399.0 11.5 copy-start.2
  4410.5 6.6 copy-start.3
Sparse Core Ops, SparseCore 0:
  2080.3 1900.0 all-reduce.4
where the time goes:
time: 4510 us
  waiting for transfers between devices  1900 us (42%)
  blocking collectives  1510 us (33%)
  matrix products  926 us (21%)
  other arithmetic  137 us (3%)
    psum x1, waiting for transfers between devices, shard_body(): totals = lax.psum(local_sums, 'data')  1900 us
    psum x1, blocking collectives, local_pass(): z_two = lax.psum(matmul(h_one, w_row[0]), 'model').astype(jnp.bfloat16)  761 us
    psum x1, blocking collectives, local_pass(): lax.psum(matmul_nt(g_three, w_col[1]), 'model').astype(jnp.bfloat16)  754 us
    dot_general x8, matrix products, exact_dot(): jnp.dot(left_mat, right_mat, precision=EXACT, preferred_element_type=jnp....  418 us
    dot_general x12, matrix products, matmul_tn(): lax.dot_general(left_mat, right_mat, TN_DIMS, preferred_element_type=jnp....  349 us
  transfers between devices with their start and end apart: 1, of which 1 were waited for; matrix products, arithmetic and copies ran while one was open for 0% of the time, Pallas kernels for 0%

commit v1 on v0

v1 whole, which is shorter than its diff:
```python
import math
import jax
import jax.numpy as jnp
from jax import lax
from jax.sharding import PartitionSpec as P

FACTOR_DECAY = 0.8
GELU_SCALE = math.sqrt(2.0 / math.pi)
GELU_CUBIC = 0.044715
EXACT = lax.Precision.HIGHEST
TN_DIMS = (((0,), (0,)), ((), ()))
NT_DIMS = (((1,), (1,)), ((), ()))
ALL_AXES = ('model', 'data')
SUB = 512
LOCAL_ORDER = ((2, 0, 1, 3), (1, 2, 3, 0))
GLOBAL_ORDER = ((1, 2, 0, 3), (3, 0, 1, 2))


def gelu_value(pre_act):
    tanh_arg = GELU_SCALE * (pre_act + GELU_CUBIC * pre_act * pre_act * pre_act)
    return 0.5 * pre_act * (1.0 + jnp.tanh(tanh_arg))


def gelu_slope(pre_act):
    tanh_arg = GELU_SCALE * (pre_act + GELU_CUBIC * pre_act * pre_act * pre_act)
    tanh_val = jnp.tanh(tanh_arg)
    return 0.5 * (1.0 + tanh_val) + 0.5 * pre_act * (1.0 - tanh_val * tanh_val) * GELU_SCALE * (1.0 + 3.0 * GELU_CUBIC * pre_act * pre_act)


def activate(pre_act):
    return gelu_value(pre_act.astype(jnp.float32)).astype(jnp.bfloat16)


def back_gate(grad_act, pre_act):
    return (grad_act.astype(jnp.float32) * gelu_slope(pre_act.astype(jnp.float32))).astype(jnp.bfloat16)


def matmul(left_mat, right_mat):
    return jnp.dot(left_mat, right_mat, preferred_element_type=jnp.float32)


def matmul_tn(left_mat, right_mat):
    return lax.dot_general(left_mat, right_mat, TN_DIMS, preferred_element_type=jnp.float32)


def matmul_nt(left_mat, right_mat):
    return lax.dot_general(left_mat, right_mat, NT_DIMS, preferred_element_type=jnp.float32)


def exact_dot(left_mat, right_mat):
    return jnp.dot(left_mat, right_mat, precision=EXACT, preferred_element_type=jnp.float32)


def exact_tn(left_mat, right_mat):
    return lax.dot_general(left_mat, right_mat, TN_DIMS, precision=EXACT, preferred_element_type=jnp.float32)


def reorder(mat, axis, order, half):
    picks = [jnp.where(half == 0, zero, one) * SUB for zero, one in zip(*order)]
    return jnp.concatenate([lax.dynamic_slice_in_dim(mat, pick, SUB, axis) for pick in picks], axis)


def full_gram_part(local_mat):
    own_a = local_mat[:, SUB:2 * SUB]
    own_b = local_mat[:, 2 * SUB:3 * SUB]
    return [matmul_tn(own_a, local_mat[:, :3 * SUB]), matmul_tn(own_b, local_mat[:, 2 * SUB:])]


def block_gram_part(own_mat):
    return [matmul_tn(own_mat[:, :SUB], own_mat), matmul_tn(own_mat[:, SUB:], own_mat[:, SUB:])]


def sum_scatter(parts):
    joined = parts[0] if len(parts) == 1 else jnp.concatenate(parts, 1)
    return lax.psum_scatter(joined, 'data', scatter_dimension=0, tiled=True)


def full_symmetric(gathered):
    def piece(half, index):
        return gathered[half * SUB:(half + 1) * SUB, index * SUB:(index + 1) * SUB]
    p02, p00, p01, p11, p13 = [piece(0, index) for index in range(5)]
    p21, p22, p23, p33, p30 = [piece(1, index) for index in range(5)]
    return jnp.concatenate([
        jnp.concatenate([p00, p01, p02, p30.T], 1),
        jnp.concatenate([p01.T, p11, p21.T, p13], 1),
        jnp.concatenate([p02.T, p21, p22, p23], 1),
        jnp.concatenate([p30, p13.T, p23.T, p33], 1),
    ], 0)


def block_symmetric(gathered):
    paa, pab, pbb = [gathered[:, index * SUB:(index + 1) * SUB] for index in range(3)]
    return jnp.concatenate([jnp.concatenate([paa, pab], 1), jnp.concatenate([pab.T, pbb], 1)], 0)


def blend_factor(old_mats, first_new, second_new, inv_rows):
    return FACTOR_DECAY * old_mats + (1.0 - FACTOR_DECAY) * inv_rows * jnp.stack([first_new, second_new])


def solution(mesh):
    data_ways = mesh.shape['data']

    def shard_body(x_tokens, dy_tokens, w_col, w_row, a_old_col, s_old_col, a_old_row, s_old_row, a_inv_col, s_inv_col, a_inv_row, s_inv_row):
        half = lax.axis_index('model')
        quarter = lax.axis_index('data')
        inv_rows = 1.0 / (x_tokens.shape[0] * data_ways)
        hidden = x_tokens.shape[1]
        own_cols = w_col.shape[2]
        piece = own_cols // data_ways

        def col_weight(layer):
            mine = lax.dynamic_slice_in_dim(w_col[layer], quarter * piece, piece, 1)
            every = lax.all_gather(mine, ALL_AXES, axis=0)
            wide = jnp.concatenate([every[index] for index in range(every.shape[0])], 1)
            return reorder(wide, 1, LOCAL_ORDER, half)

        def row_weight(layer):
            mine = lax.dynamic_slice_in_dim(w_row[layer], quarter * piece, piece, 0)
            every = lax.all_gather(mine, ALL_AXES, axis=0, tiled=True)
            return reorder(every, 0, LOCAL_ORDER, half)

        weight_one = col_weight(0)
        weight_two = reorder(row_weight(0), 1, LOCAL_ORDER, half)
        weight_three = reorder(col_weight(1), 0, LOCAL_ORDER, half)
        weight_four = row_weight(1)
        own = slice(SUB, 3 * SUB)

        x_local = reorder(x_tokens, 1, LOCAL_ORDER, half)
        dy_local = reorder(dy_tokens, 1, LOCAL_ORDER, half)
        edge_sum = sum_scatter(full_gram_part(x_local) + full_gram_part(dy_local))

        z_one = matmul(x_tokens, weight_one).astype(jnp.bfloat16)
        h_one = activate(z_one)
        h_one_own = h_one[:, own]
        z_two = matmul(h_one, weight_two).astype(jnp.bfloat16)
        h_two = activate(z_two)
        early_sum = sum_scatter(block_gram_part(h_one_own) + full_gram_part(h_two))
        z_three = matmul(h_two, weight_three).astype(jnp.bfloat16)
        h_three_own = activate(z_three[:, own])
        dw_four = sum_scatter([matmul_tn(h_three_own, dy_tokens)])
        g_three = back_gate(matmul_nt(dy_tokens, weight_four).astype(jnp.bfloat16), z_three)
        g_three_own = g_three[:, own]
        middle_sum = sum_scatter(block_gram_part(h_three_own) + block_gram_part(g_three_own))
        dw_three = sum_scatter([matmul_tn(g_three_own, h_two)])
        g_two = back_gate(matmul_nt(g_three, weight_three).astype(jnp.bfloat16), z_two)
        dw_two = sum_scatter([matmul_tn(h_one_own, g_two)])
        g_one_own = back_gate(matmul_nt(g_two, weight_two[own]).astype(jnp.bfloat16), z_one[:, own])
        dw_one = sum_scatter([matmul_tn(g_one_own, x_tokens)])
        late_sum = sum_scatter(full_gram_part(g_two) + block_gram_part(g_one_own))

        def half_done(grad_piece, inverse, is_local):
            if is_local:
                grad_piece = reorder(grad_piece, 1, GLOBAL_ORDER, half)
            done = exact_dot(grad_piece * inv_rows, inverse)
            return lax.all_gather(done, 'data', axis=0, tiled=True)

        u_row_four = exact_dot(a_inv_row[1], half_done(dw_four, s_inv_row[1], False))
        u_col_three = exact_tn(half_done(dw_three, a_inv_col[1], True), s_inv_col[1])
        u_row_two = exact_dot(a_inv_row[0], half_done(dw_two, s_inv_row[0], True))
        u_col_one = exact_tn(half_done(dw_one, a_inv_col[0], False), s_inv_col[0])
        u_col = jnp.stack([u_col_one, u_col_three])
        u_row = jnp.stack([u_row_two, u_row_four])

        full_cols = 5 * SUB
        block_cols = 3 * SUB
        edge_all = lax.all_gather(edge_sum, ALL_AXES, axis=0, tiled=True)
        h_two_all = lax.all_gather(early_sum[:, block_cols:], ALL_AXES, axis=0, tiled=True)
        g_two_all = lax.all_gather(late_sum[:, :full_cols], ALL_AXES, axis=0, tiled=True)
        middle_all = lax.all_gather(middle_sum, 'data', axis=0, tiled=True)
        outer_all = lax.all_gather(jnp.concatenate([early_sum[:, :block_cols], late_sum[:, full_cols:]], 1), 'data', axis=0, tiled=True)

        a_new_col = blend_factor(a_old_col, full_symmetric(edge_all[:, :full_cols]), full_symmetric(h_two_all), inv_rows)
        s_new_row = blend_factor(s_old_row, full_symmetric(g_two_all), full_symmetric(edge_all[:, full_cols:]), inv_rows)
        a_new_row = blend_factor(a_old_row, block_symmetric(outer_all[:, :block_cols]), block_symmetric(middle_all[:, :block_cols]), inv_rows)
        s_new_col = blend_factor(s_old_col, block_symmetric(outer_all[:, block_cols:]), block_symmetric(middle_all[:, block_cols:]), inv_rows)
        return (u_col, u_row, a_new_col, s_new_col, a_new_row, s_new_row)

    batch_split = P('data', None)
    col_split = P(None, None, 'model')
    row_split = P(None, 'model', None)
    replicated = P()
    return jax.shard_map(
        shard_body,
        mesh=mesh,
        in_specs=(batch_split, batch_split, col_split, row_split, replicated, row_split, row_split, replicated, replicated, row_split, row_split, replicated),
        out_specs=(col_split, row_split, replicated, row_split, row_split, replicated),
        check_vma=False,
    )
```

time: 4510 us -> 1870 us (0.41)
  blocking collectives: 1510 us -> 0 us
  waiting for transfers between devices: 1900 us -> 558 us
  local copies, waits for them, and re-layouts: 12.6 us -> 237 us
  matrix products: 926 us -> 802 us
  other arithmetic: 137 us -> 247 us
    psum x1 -> x0, waiting for transfers between devices: 1900 us -> none  [shard_body(): totals = lax.psum(local_sums, 'data')]
    psum x2 -> x0, blocking collectives: 1510 us -> none  [the longest x1 761 us: local_pass(): z_two = lax.psum(matmul(h_one, w_row[0]), 'model').astype(jnp.bfloat16)]
    all_gather x0 -> x13, waiting for transfers between devices: none -> 357 us  [the longest x2 90.9 us: row_weight(): every = lax.all_gather(mine, ALL_AXES, axis=0, tiled=True)]
    dot_general x8 -> x6, matrix products: 418 us -> 187 us  [exact_dot(): jnp.dot(left_mat, right_mat, precision=EXACT, preferred_element_type=jnp....]
    reduce_scatter x0 -> x8, waiting for transfers between devices: none -> 200 us  [sum_scatter(): return lax.psum_scatter(joined, 'data', scatter_dimension=0, tiled=True)]
    dot_general x12 -> x20, matrix products: 349 us -> 224 us  [matmul_tn(): lax.dot_general(left_mat, right_mat, TN_DIMS, preferred_element_type=jnp....]
    another operation x2 -> x10, other arithmetic: 15.1 us -> 115 us  [the longest x8 101 us: blend_factor(): jnp.stack([first_new, second_new])]
    dot_general x3, matrix products: 68.8 us -> 164 us  [matmul(): return jnp.dot(left_mat, right_mat, preferred_element_type=jnp.float32)]
  transfers between devices with their start and end apart: 1 -> 21, of which waited for: 1 -> 15; matrix products, arithmetic and copies ran while one was open for 0% -> 40% of each run, Pallas kernels for 0% -> 0%
where the time goes in v1:
time: 1870 us; the launch traced here: 1860 us
  matrix products  802 us (43%)
  waiting for transfers between devices  558 us (30%)
  other arithmetic  247 us (13%)
  local copies, waits for them, and re-layouts  237 us (13%)
    dot_general x20, matrix products, matmul_tn(): lax.dot_general(left_mat, right_mat, TN_DIMS, preferred_element_type=jnp....  224 us
    reduce_scatter x8, waiting for transfers between devices, sum_scatter(): return lax.psum_scatter(joined, 'data', scatter_dimension=0, tiled=True)  200 us
    dot_general x6, matrix products, exact_dot(): jnp.dot(left_mat, right_mat, precision=EXACT, preferred_element_type=jnp....  187 us
    dot_general x3, matrix products, matmul_nt(): lax.dot_general(left_mat, right_mat, NT_DIMS, preferred_element_type=jnp....  165 us
    dot_general x3, matrix products, matmul(): return jnp.dot(left_mat, right_mat, preferred_element_type=jnp.float32)  164 us
    another operation x8, other arithmetic, blend_factor(): jnp.stack([first_new, second_new])  101 us
    all_gather x2, waiting for transfers between devices, row_weight(): every = lax.all_gather(mine, ALL_AXES, axis=0, tiled=True)  90.9 us
    unnamed x105, local copies, waits for them, and re-layouts  83.8 us
  transfers between devices with their start and end apart: 21, of which 15 were waited for; matrix products, arithmetic and copies ran while one was open for 40% of the time, Pallas kernels for 0%

profile of v1, /device:TPU:0, one launch (start us, length us, event | category | flops | bytes accessed | tf_op | source)
XLA Modules:
  0.0 1860.4 jit_solution(14151719565010712279)
XLA Ops:
  7.2 6.1 fusion.200
  26.9 40.1 %all-gather.40.cloned.1.call-done = bf16[1,2048,2048]{2,1,0:T(8,128)(2,1)} async-done(((bf16[1,256,2048]{2,1,0:T(8,128)(2,1)}), bf16[1,2048,2048]{2,1,0:T(8,128)(2,1)}) %all-gather.40.cloned.1.call-update) | async-done | bytes 8388624 | tf_op jit(solution)/shard_map/all_gather | solution.py:119
  67.0 50.8 %all-gather.38.cloned.1.call-done = bf16[1,2048,2048]{2,1,0:T(8,128)(2,1)} async-done(((bf16[1,256,2048]{2,1,0:T(8,128)(2,1)}), bf16[1,2048,2048]{2,1,0:T(8,128)(2,1)}) %all-gather.38.cloned.1.call-update) | async-done | bytes 8388624 | tf_op jit(solution)/shard_map/all_gather | solution.py:119
  117.8 10.1 dynamic-slice_bitcast_fusion.3
  132.7 35.8 %all-gather.18.cloned.1.call-done = bf16[8,2048,256]{2,1,0:T(8,128)(2,1)} async-done(((bf16[1,2048,256]{2,1,0:T(8,128)(2,1)}), bf16[8,2048,256]{2,1,0:T(8,128)(2,1)}) %all-gather.18.cloned.1.call-update) | async-done | bytes 8388624 | tf_op jit(solution)/shard_map/all_gather | solution.py:113
  186.6 32.5 %all-gather.16.cloned.1.call-done = bf16[8,2048,256]{2,1,0:T(8,128)(2,1)} async-done(((bf16[1,2048,256]{2,1,0:T(8,128)(2,1)}), bf16[8,2048,256]{2,1,0:T(8,128)(2,1)}) %all-gather.16.cloned.1.call-update) | async-done | bytes 8388624 | tf_op jit(solution)/shard_map/all_gather | solution.py:113
  230.1 6.5 constant_dynamic-slice_fusion.23
  250.1 53.9 %fusion.9 = (bf16[4096,2048]{0,1:T(8,128)(2,1)}, bf16[4096,2048]{0,1:T(8,128)(2,1)}) fusion(bf16[4096,2048]{1,0:T(8,128)(2,1)} %param.12, bf16[2048,2048]{1,0:T(8,128)(2,1)} %fusion.87.clone.4), kind=kOutput, calls=%fused_computation.35 | convolution fusion | flops 34452013056 | bytes 58720256 | tf_op jit(solution)/shard_map/dot_general | solution.py:39
  304.0 6.6 fusion.73.clone.5
  310.6 66.8 %fusion.2 = (bf16[4096,2048]{0,1:T(8,128)(2,1)}, bf16[4096,2048]{0,1:T(8,128)(2,1)}) fusion(bf16[4096,2048]{0,1:T(8,128)(2,1)} %get-tuple-element.118, bf16[2048,2048]{1,0:T(8,128)(2,1)} %fusion.73.clone.5), kind=kOutput, calls=%fused_computation.28 | convolution fusion | flops 34535899136 | bytes 58720256 | tf_op jit(solution)/shard_map/dot_general | solution.py:39
  377.4 43.7 %convolution_convert_fusion = bf16[4096,2048]{0,1:T(8,128)(2,1)S(1)} fusion(bf16[4096,2048]{0,1:T(8,128)(2,1)} %get-tuple-element.115, bf16[512,2048]{1,0:T(8,128)(2,1)} %get-tuple-element.74, bf16[512,2048]{1,0:T(8,128)(2,1)} %get-tuple-element.75, bf16[512,2048]{1,0:T(8,128)(2,1)} %get-tuple-element.76, bf16[512,2048]{1,0:T(8,128)(2,1)S(1)} %copy-done.26), kind=kOutput, calls=%fused_computation.93 | convolution fusion | flops 34401681408 | bytes 41943040 | tf_op jit(solution)/shard_map/dot_general | solution.py:39
  421.2 8.2 fusion.28
  436.3 63.3 %fusion.23 = bf16[4096,2048]{0,1:T(8,128)(2,1)} fusion(bf16[4096,2048]{0,1:T(8,128)(2,1)} %copy-done.20, bf16[4096,2048]{1,0:T(8,128)(2,1)} %param.13, bf16[2048,2048]{1,0:T(8,128)(2,1)} %fusion.236), kind=kOutput, calls=%fused_computation.49 | convolution fusion | flops 34544287744 | bytes 58720256 | tf_op jit(solution)/shard_map/dot_general | solution.py:47
  499.7 6.0 fusion.112
  505.6 10.6 fusion.108
  519.6 5.9 fusion.117
  525.5 65.1 %fusion.7 = bf16[4096,2048]{0,1:T(8,128)(2,1)} fusion(bf16[4096,2048]{0,1:T(8,128)(2,1)} %get-tuple-element.116, bf16[4096,2048]{0,1:T(8,128)(2,1)} %fusion.23, bf16[512,2048]{1,0:T(8,128)(2,1)} %get-tuple-element.74, bf16[512,2048]{1,0:T(8,128)(2,1)} %get-tuple-element.75, bf16[512,2048]{1,0:T(8,128)(2,1)} %get-tuple-element.76, ...), kind=kOutput, calls=%fused_computation.33 | convolution fusion | flops 34577842176 | bytes 58720256 | tf_op jit(solution)/shard_map/dot_general | solution.py:47
  595.8 36.8 %fusion.39 = bf16[4096,1024]{0,1:T(8,128)(2,1)} fusion(bf16[4096,2048]{0,1:T(8,128)(2,1)} %get-tuple-element.118, bf16[4096,2048]{0,1:T(8,128)(2,1)} %fusion.7, bf16[2048,512]{1,0:T(8,128)(2,1)} %get-tuple-element.88, bf16[2048,512]{1,0:T(8,128)(2,1)} %get-tuple-element.89, bf16[2048,512]{1,0:T(8,128)(2,1)} %get-tuple-element.90, ...), kind=kOutput, calls=%fused_computation.72 | convolution fusion | flops 17288921088 | bytes 41943040 | tf_op jit(solution)/shard_map/dot_general | solution.py:47
  632.6 6.0 fusion.119
  643.1 9.3 fusion.69
  652.5 10.6 fusion.53
  672.8 9.4 fusion.71
  682.2 9.3 fusion.104
  691.5 10.6 fusion.55
  705.8 24.1 %fusion.207 = f32[1024,2048]{1,0:T(8,128)} fusion(bf16[4096,1024]{0,1:T(8,128)(2,1)} %fusion.28, bf16[4096,2048]{1,0:T(8,128)(2,1)} %param.13), kind=kOutput, calls=%fused_computation.338 | convolution fusion | flops 17179869184 | bytes 33554432 | tf_op jit(solution)/shard_map/dot_general | solution.py:43
  730.3 24.2 %fusion.106 = f32[1024,2048]{1,0:T(8,128)} fusion(bf16[4096,2048]{0,1:T(8,128)(2,1)} %fusion.7, bf16[4096,2048]{0,1:T(8,128)(2,1)} %get-tuple-element.117), kind=kOutput, calls=%fused_computation.156 | convolution fusion | flops 17179869184 | bytes 33554432 | tf_op jit(solution)/shard_map/dot_general | solution.py:43
  754.6 24.1 %fusion.110 = f32[1024,2048]{1,0:T(8,128)} fusion(bf16[4096,2048]{0,1:T(8,128)(2,1)} %get-tuple-element.115, bf16[4096,2048]{0,1:T(8,128)(2,1)} %fusion.23), kind=kOutput, calls=%fused_computation.160 | convolution fusion | flops 17179869184 | bytes 33554432 | tf_op jit(solution)/shard_map/dot_general | solution.py:43
  778.8 24.0 %fusion.206 = f32[1024,2048]{1,0:T(8,128)} fusion(bf16[4096,1024]{0,1:T(8,128)(2,1)} %fusion.39, bf16[4096,2048]{1,0:T(8,128)(2,1)} %param.12), kind=kOutput, calls=%fused_computation.337 | convolution fusion | flops 17179869184 | bytes 33554432 | tf_op jit(solution)/shard_map/dot_general | solution.py:43
  803.1 8.6 constant_dynamic-slice_fusion.2
  811.7 12.5 constant_dynamic-slice_fusion.6
  824.2 9.6 fusion.98
  839.6 9.0 fusion.63
  848.6 11.7 fusion.57
  870.5 18.6 %fusion.41 = f32[256,2048]{1,0:T(8,128)} fusion(f32[2,2048,2048]{2,1,0:T(8,128)} %param.23, f32[256,2048]{1,0:T(8,128)} %reduce-scatter.15.cloned.1.call-done), kind=kOutput, calls=%fused_computation.80 | convolution fusion | flops 12885426176 | bytes 20971520 | tf_op jit(solution)/shard_map/dot_general | solution.py:51
  889.2 45.8 %reduce-scatter.13.cloned.1.call-done = f32[256,2048]{1,0:T(8,128)} async-done(((f32[1024,2048]{1,0:T(8,128)}), f32[256,2048]{1,0:T(8,128)}) %reduce-scatter.13.cloned.1.call-update) | async-done | bytes 2097168 | tf_op jit(solution)/shard_map/reduce_scatter | solution.py:75
  936.7 18.1 fusion.43
  954.9 48.2 %reduce-scatter.11.cloned.1.call-done = f32[256,2048]{1,0:T(8,128)} async-done(((f32[1024,2048]{1,0:T(8,128)}), f32[256,2048]{1,0:T(8,128)}) %reduce-scatter.11.cloned.1.call-update) | async-done | bytes 2097168 | tf_op jit(solution)/shard_map/reduce_scatter | solution.py:75
  1004.8 18.5 fusion.45
  1023.4 48.0 %reduce-scatter.9.cloned.1.call-done = f32[256,2048]{1,0:T(8,128)} async-done(((f32[1024,2048]{1,0:T(8,128)}), f32[256,2048]{1,0:T(8,128)}) %reduce-scatter.9.cloned.1.call-update) | async-done | bytes 2097168 | tf_op jit(solution)/shard_map/reduce_scatter | solution.py:75
  1071.3 18.6 fusion.47
  1093.9 58.4 %reduce-scatter.17.cloned.1.call-done = f32[128,5120]{1,0:T(8,128)} async-done(((f32[512,5120]{1,0:T(8,128)}), f32[128,5120]{1,0:T(8,128)}) %reduce-scatter.17.cloned.1.call-update) | async-done | bytes 2621456 | tf_op jit(solution)/shard_map/reduce_scatter | solution.py:75
  1152.3 45.2 %all-gather.34.cloned.1.call-done = f32[512,3072]{1,0:T(8,128)} async-done(((f32[128,3072]{1,0:T(8,128)}), f32[512,3072]{1,0:T(8,128)}) %all-gather.34.cloned.1.call-update) | async-done | bytes 6291472 | tf_op jit(solution)/shard_map/all_gather | solution.py:169
  1209.7 33.4 %all-gather.32.cloned.1.call-done = f32[512,3072]{1,0:T(8,128)} async-done(((f32[128,3072]{1,0:T(8,128)}), f32[512,3072]{1,0:T(8,128)}) %all-gather.32.cloned.1.call-update) | async-done | bytes 6291472 | tf_op jit(solution)/shard_map/all_gather | solution.py:170
  1258.8 6.6 fusion.103
  1265.4 34.8 %all-gather.26.cloned.1.call-done = f32[1024,2048]{1,0:T(8,128)} async-done(((f32[256,2048]{1,0:T(8,128)}), f32[1024,2048]{1,0:T(8,128)}) %all-gather.26.cloned.1.call-update) | async-done | bytes 8388624 | tf_op jit(solution)/shard_map/all_gather | solution.py:155
  1300.2 57.5 %convolution_bitcast_fusion = f32[1,1024,2048]{1,2,0:T(8,128)} fusion(f32[1024,2048]{1,0:T(8,128)} %all-gather.26.cloned.1.call-done, f32[2,1024,1024]{2,1,0:T(8,128)} %param.22), kind=kOutput, calls=%fused_computation.163 | convolution fusion | flops 25769803776 | bytes 20971520 | tf_op jit(solution)/shard_map/dot_general | solution.py:51
  1357.7 55.9 %convolution_bitcast_fusion.1 = f32[1,1024,2048]{1,2,0:T(8,128)S(1)} fusion(f32[1024,2048]{1,0:T(8,128)} %all-gather.24.cloned.1.call-done, f32[2,1024,1024]{2,1,0:T(8,128)} %param.22), kind=kOutput, calls=%fused_computation.164 | convolution fusion | flops 25769803776 | bytes 20971520 | tf_op jit(solution)/shard_map/dot_general | solution.py:51
  1413.6 6.6 pad_maximum_fusion.1
  1420.2 17.3 copy.103
  1437.6 31.2 %convolution_bitcast_fusion.2 = f32[1,2048,1024]{2,1,0:T(8,128)} fusion(f32[1024,2048]{1,0:T(8,128)} %all-gather.22.cloned.1.call-done, f32[2,1024,1024]{2,1,0:T(8,128)} %param.21), kind=kOutput, calls=%fused_computation.165 | convolution fusion | flops 25769803776 | bytes 20971520 | tf_op jit(solution)/shard_map/dot_general | solution.py:55
  1472.7 30.0 %convolution_bitcast_fusion.3 = f32[1,2048,1024]{2,1,0:T(8,128)S(1)} fusion(f32[1024,2048]{1,0:T(8,128)} %all-gather.20.cloned.1.call-done, f32[2,1024,1024]{2,1,0:T(8,128)} %param.21), kind=kOutput, calls=%fused_computation.166 | convolution fusion | flops 25769803776 | bytes 20971520 | tf_op jit(solution)/shard_map/dot_general | solution.py:55
  1502.8 6.8 pad_maximum_fusion
  1509.6 22.3 %all-gather.30.cloned.1.call-done = f32[1024,2560]{1,0:T(8,128)} async-done(((f32[128,2560]{1,0:T(8,128)}), f32[1024,2560]{1,0:T(8,128)}) %all-gather.30.cloned.1.call-update) | async-done | bytes 10485776 | tf_op jit(solution)/shard_map/all_gather | solution.py:167
  1532.0 6.7 slice_bitcast_fusion.23
  1550.2 40.8 %all-gather.36.cloned.1.call-done = f32[1024,2560]{1,0:T(8,128)} async-done(((f32[128,2560]{1,0:T(8,128)}), f32[1024,2560]{1,0:T(8,128)}) %all-gather.36.cloned.1.call-update) | async-done | bytes 10485776 | tf_op jit(solution)/shard_map/all_gather | solution.py:168
  1591.0 6.7 fusion.199
  1618.2 27.6 %maximum_bitcast_fusion.2 = f32[1,2048,2048]{2,1,0:T(8,128)} fusion(f32[512,512]{1,0:T(8,128)} %get-tuple-element.55, f32[512,512]{1,0:T(8,128)} %bitcast.216, f32[512,512]{1,0:T(8,128)} %copy.94, f32[512,512]{1,0:T(8,128)S(1)} %get-tuple-element.51, f32[512,1536]{1,0:T(8,128)S(1)} %slice.549, f32[512,512]{1,0:T(8,128)} %bitcast.217, ...), kind=kLoop, calls=%fused_computation.78 | loop fusion | flops 50331648 | bytes 33554432 | tf_op jit(solution)/shard_map/stack | solution.py:97
  1645.8 31.6 %maximum_bitcast_fusion.1 = f32[1,2048,2048]{2,1,0:T(8,128)} fusion(f32[512,512]{1,0:T(8,128)S(1)} %copy-done.18, f32[512,512]{1,0:T(8,128)} %copy.79, f32[512,512]{1,0:T(8,128)} %copy.78, f32[512,512]{1,0:T(8,128)} %get-tuple-element.65, f32[512,1536]{1,0:T(8,128)S(1)} %slice.518, f32[512,512]{1,0:T(8,128)} %bitcast.206, f32[512,512]{1,0:T(8,128)S(1)} %copy-done.16, ...), kind=kLoop, calls=%fused_computation.77 | loop fusion | flops 50331648 | bytes 33554432 | tf_op jit(solution)/shard_map/stack | solution.py:97
  1677.4 17.3 all-gather.28.cloned.1.call-done
  1694.7 12.0 fusion.197
  1750.6 19.8 %maximum_bitcast_fusion = f32[1,2048,2048]{2,1,0:T(8,128)} fusion(f32[512,512]{1,0:T(8,128)} %get-tuple-element.31, f32[512,512]{1,0:T(8,128)} %bitcast.213, f32[512,512]{1,0:T(8,128)} %bitcast.201, f32[512,512]{1,0:T(8,128)} %get-tuple-element.36, f32[512,1536]{1,0:T(8,128)} %get-tuple-element.39, f32[512,512]{1,0:T(8,128)} %bitcast.215, ...), kind=kLoop, calls=%fused_computation.76 | loop fusion | flops 37748736 | bytes 33554432 | tf_op jit(solution)/shard_map/stack | solution.py:97
  1770.4 33.2 %fusion.25 = f32[2,2048,2048]{2,1,0:T(8,128)} fusion(f32[1,2048,2048]{2,1,0:T(8,128)} %maximum_bitcast_fusion.1, f32[1,2048,2048]{2,1,0:T(8,128)} %maximum_bitcast_fusion, f32[2,2048,2048]{2,1,0:T(8,128)} %param.16), kind=kLoop, calls=%fused_computation.52 | loop fusion | flops 33554432 | bytes 100663296 | tf_op jit(solution)/shard_map/add | solution.py:97
  1803.6 16.6 maximum_bitcast_fusion.3
  1820.2 33.2 %fusion.26 = f32[2,2048,2048]{2,1,0:T(8,128)} fusion(f32[1,2048,2048]{2,1,0:T(8,128)} %maximum_bitcast_fusion.3, f32[1,2048,2048]{2,1,0:T(8,128)} %maximum_bitcast_fusion.2, f32[2,2048,2048]{2,1,0:T(8,128)} %param.19), kind=kLoop, calls=%fused_computation.54 | loop fusion | flops 33554432 | bytes 100663296 | tf_op jit(solution)/shard_map/add | solution.py:97
  (207 shorter events, 226.0 us)
Async XLA Ops:
  7.2 59.8 %all-gather.40.cloned.1.call-start = ((), (), s32[]{:S(2)}) async-start(), calls=%async_computation.28 | async-start | bytes 9437184 | tf_op jit(solution)/shard_map/all_gather | solution.py:119
  15.7 102.1 %all-gather.38.cloned.1.call-start = ((), (), s32[]{:S(2)}) async-start(), calls=%async_computation.27 | async-start | bytes 9437184 | tf_op jit(solution)/shard_map/all_gather | solution.py:119
  18.1 150.5 %all-gather.18.cloned.1.call-start = ((), (), s32[]{:S(2)}) async-start(), calls=%async_computation.9 | async-start | bytes 9437184 | tf_op jit(solution)/shard_map/all_gather | solution.py:113
  24.5 194.6 %all-gather.16.cloned.1.call-start = ((), (), s32[]{:S(2)}) async-start(), calls=%async_computation.8 | async-start | bytes 9437184 | tf_op jit(solution)/shard_map/all_gather | solution.py:113
  26.8 839.1 %reduce-scatter.23.cloned.1.call-start = ((), (), s32[]{:S(2)}) async-start(), calls=%async_computation.24 | async-start | bytes 7864320 | tf_op jit(solution)/shard_map/reduce_scatter | solution.py:75
  132.7 171.3 %copy-start.7 = (bf16[2048,512]{1,0:T(8,128)(2,1)}, bf16[2048,512]{1,0:T(8,128)(2,1)S(1)}, u32[]{:S(2)}) copy-start(bf16[2048,512]{1,0:T(8,128)(2,1)S(1)} %get-tuple-element.87) | copy-start | bytes 6291460
  310.6 66.8 %copy-start.26 = (bf16[512,2048]{1,0:T(8,128)(2,1)S(1)}, bf16[512,2048]{1,0:T(8,128)(2,1)}, u32[]{:S(2)}) copy-start(bf16[512,2048]{1,0:T(8,128)(2,1)} %get-tuple-element.73) | copy-start | bytes 6291460
  421.2 11.1 copy-start.20
  421.2 11.1 copy-start.9
  421.2 11.1 copy-start.10
  421.2 11.1 copy-start.11
  421.2 11.1 copy-start.12
  499.6 16.6 slice-start.2
  505.6 10.7 slice-start.3
  519.6 5.9 copy-start.27
  590.6 5.2 copy-start.8
  595.7 271.0 %reduce-scatter.21.cloned.1.call-start = ((), (), s32[]{:S(2)}) async-start(), calls=%async_computation.22 | async-start | bytes 10485760 | tf_op jit(solution)/shard_map/reduce_scatter | solution.py:75
  632.6 6.0 copy-start.30
  666.7 201.3 %reduce-scatter.19.cloned.1.call-start = ((), (), s32[]{:S(2)}) async-start(), calls=%async_computation.20 | async-start | bytes 10485760 | tf_op jit(solution)/shard_map/reduce_scatter | solution.py:75
  705.7 164.8 %reduce-scatter.15.cloned.1.call-start = ((), (), s32[]{:S(2)}) async-start(), calls=%async_computation.16 | async-start | bytes 10485760 | tf_op jit(solution)/shard_map/reduce_scatter | solution.py:75
  729.9 205.1 %reduce-scatter.13.cloned.1.call-start = ((), (), s32[]{:S(2)}) async-start(), calls=%async_computation.14 | async-start | bytes 10485760 | tf_op jit(solution)/shard_map/reduce_scatter | solution.py:75
  754.6 248.5 %reduce-scatter.11.cloned.1.call-start = ((), (), s32[]{:S(2)}) async-start(), calls=%async_computation.12 | async-start | bytes 10485760 | tf_op jit(solution)/shard_map/reduce_scatter | solution.py:75
  778.8 292.6 %reduce-scatter.9.cloned.1.call-start = ((), (), s32[]{:S(2)}) async-start(), calls=%async_computation.10 | async-start | bytes 10485760 | tf_op jit(solution)/shard_map/reduce_scatter | solution.py:75
  802.8 349.4 %reduce-scatter.17.cloned.1.call-start = ((), (), s32[]{:S(2)}) async-start(), calls=%async_computation.18 | async-start | bytes 13107200 | tf_op jit(solution)/shard_map/reduce_scatter | solution.py:75
  811.7 12.6 copy-start.13
  824.2 9.6 copy-start.14
  824.2 9.6 copy-start.15
  848.6 11.7 copy-start.25
  848.6 11.7 copy-start.28
  865.9 331.5 %all-gather.34.cloned.1.call-start = ((), (), s32[]{:S(2)}) async-start(), calls=%async_computation.25 | async-start | bytes 7864320 | tf_op jit(solution)/shard_map/all_gather | solution.py:169
  866.7 376.4 %all-gather.32.cloned.1.call-start = ((), (), s32[]{:S(2)}) async-start(), calls=%async_computation.23 | async-start | bytes 7864320 | tf_op jit(solution)/shard_map/all_gather | solution.py:170
  870.4 429.7 %all-gather.26.cloned.1.call-start = ((), (), s32[]{:S(2)}) async-start(), calls=%async_computation.17 | async-start | bytes 10485760 | tf_op jit(solution)/shard_map/all_gather | solution.py:155
  889.1 468.5 %all-gather.24.cloned.1.call-start = ((), (), s32[]{:S(2)}) async-start(), calls=%async_computation.15 | async-start | bytes 10485760 | tf_op jit(solution)/shard_map/all_gather | solution.py:155
  954.8 482.7 %all-gather.22.cloned.1.call-start = ((), (), s32[]{:S(2)}) async-start(), calls=%async_computation.13 | async-start | bytes 10485760 | tf_op jit(solution)/shard_map/all_gather | solution.py:155
  1023.3 69.3 %copy-start.29 = (f32[128,4096]{1,0:T(8,128)S(1)}, f32[128,4096]{1,0:T(8,128)}, u32[]{:S(2)}) copy-start(f32[128,4096]{1,0:T(8,128)} %reduce-scatter.21.cloned.1.call-done) | copy-start | bytes 6291460
  1023.3 449.4 %all-gather.20.cloned.1.call-start = ((), (), s32[]{:S(2)}) async-start(), calls=%async_computation.11 | async-start | bytes 10485760 | tf_op jit(solution)/shard_map/all_gather | solution.py:155
  1089.9 442.0 %all-gather.30.cloned.1.call-start = ((), (), s32[]{:S(2)}) async-start(), calls=%async_computation.21 | async-start | bytes 11796480 | tf_op jit(solution)/shard_map/all_gather | solution.py:167
  1092.5 498.5 %all-gather.36.cloned.1.call-start = ((), (), s32[]{:S(2)}) async-start(), calls=%async_computation.26 | async-start | bytes 11796480 | tf_op jit(solution)/shard_map/all_gather | solution.py:168
  1093.8 600.9 %all-gather.28.cloned.1.call-start = ((), (), s32[]{:S(2)}) async-start(), calls=%async_computation.19 | async-start | bytes 23592960 | tf_op jit(solution)/shard_map/all_gather | solution.py:166
  1202.2 2.7 copy-start.23
  1202.2 5.1 copy-start.21
  1247.6 2.7 copy-start.24
  1247.7 3.3 copy-start.22
  1247.7 4.1 slice-start
  1250.4 2.8 copy-start
  1250.4 4.0 slice-start.1
  1254.4 4.4 copy-start.1
  1357.7 56.0 %copy-start.5 = (f32[1,1024,2048]{1,2,0:T(8,128)S(1)}, f32[1,1024,2048]{1,2,0:T(8,128)}, u32[]{:S(2)}) copy-start(f32[1,1024,2048]{1,2,0:T(8,128)} %convolution_bitcast_fusion) | copy-start | bytes 25165828
  1472.7 30.1 %copy-start.6 = (f32[1,2048,1024]{2,1,0:T(8,128)S(1)}, f32[1,2048,1024]{2,1,0:T(8,128)}, u32[]{:S(2)}) copy-start(f32[1,2048,1024]{2,1,0:T(8,128)} %convolution_bitcast_fusion.2) | copy-start | bytes 25165828
  1618.2 27.6 %copy-start.16 = (f32[512,512]{1,0:T(8,128)S(1)}, f32[512,512]{1,0:T(8,128)}, u32[]{:S(2)}) copy-start(f32[512,512]{1,0:T(8,128)} %get-tuple-element.61) | copy-start | bytes 3145732
  1618.2 27.6 %copy-start.17 = (f32[512,512]{1,0:T(8,128)S(1)}, f32[512,512]{1,0:T(8,128)}, u32[]{:S(2)}) copy-start(f32[512,512]{1,0:T(8,128)} %get-tuple-element.63) | copy-start | bytes 3145732
  1618.2 27.6 %copy-start.18 = (f32[512,512]{1,0:T(8,128)S(1)}, f32[512,512]{1,0:T(8,128)}, u32[]{:S(2)}) copy-start(f32[512,512]{1,0:T(8,128)} %get-tuple-element.64) | copy-start | bytes 3145732
  1706.7 14.4 copy-start.4
  1706.7 27.6 %copy-start.3 = (f32[512,512]{1,0:T(8,128)}, f32[512,512]{1,0:T(8,128)S(1)}, u32[]{:S(2)}) copy-start(f32[512,512]{1,0:T(8,128)S(1)} %get-tuple-element.25) | copy-start | bytes 3145732
  1706.7 32.7 %copy-start.2 = (f32[512,512]{1,0:T(8,128)}, f32[512,512]{1,0:T(8,128)S(1)}, u32[]{:S(2)}) copy-start(f32[512,512]{1,0:T(8,128)S(1)} %get-tuple-element.24) | copy-start | bytes 3145732
  1726.6 11.5 copy-start.19
Sparse Core Ops, SparseCore 0:
  15.8 51.1 all-gather.39
  69.4 48.3 all-gather.37
  120.2 48.3 all-gather.17
  170.8 48.3 all-gather.15
  595.9 51.3 reduce-scatter.22
  666.8 65.1 reduce-scatter.20
  734.5 65.0 reduce-scatter.18
  802.2 65.0 reduce-scatter.14
  869.9 65.0 reduce-scatter.12
  938.0 65.0 reduce-scatter.10
  1006.2 65.0 reduce-scatter.8
  1074.3 77.8 reduce-scatter.16
  1153.8 43.6 all-gather.33
  1199.4 43.5 all-gather.31
  1244.4 55.7 all-gather.25
  1301.5 55.7 all-gather.23
  1359.2 55.7 all-gather.21
  1417.0 55.7 all-gather.19
  1474.5 57.3 all-gather.29
  1533.6 57.3 all-gather.35
  1592.9 101.8 all-gather.27

commit v2 on v0

v2 whole, which is shorter than its diff:
```python
import functools
import math
import jax
import jax.numpy as jnp
from jax import lax
from jax.experimental import pallas as pl
from jax.experimental.pallas import tpu as pltpu
from jax.sharding import PartitionSpec as P

FACTOR_DECAY = 0.8
GELU_SCALE = math.sqrt(2.0 / math.pi)
GELU_CUBIC = 0.044715
EXACT = lax.Precision.HIGHEST
TN_DIMS = (((0,), (0,)), ((), ()))
NT_DIMS = (((1,), (1,)), ((), ()))
SUB = 512
OWN = slice(SUB, 3 * SUB)
LOCAL_ORDER = ((2, 0, 1, 3), (1, 2, 3, 0))
MODEL_SWAP = ((0, 1), (1, 0))
CHIP_SWAP = ((0, 2), (2, 0), (1, 3), (3, 1))
CORE_SWAP = ((0, 1), (1, 0), (2, 3), (3, 2))
FULL_TABLE = ((0, 1, 0), (0, 2, 0), (0, 0, 0), (1, 4, 1),
              (0, 2, 1), (0, 3, 0), (1, 0, 1), (0, 4, 0),
              (0, 0, 1), (1, 0, 0), (1, 1, 0), (1, 2, 0),
              (1, 4, 0), (0, 4, 1), (1, 2, 1), (1, 3, 0))
BLOCK_TABLE = ((0, 0, 0), (0, 1, 0), (0, 1, 1), (0, 2, 0))


def gelu_value(pre_act):
    tanh_val = jnp.tanh(pre_act * (GELU_SCALE + (GELU_SCALE * GELU_CUBIC * pre_act) * pre_act))
    return 0.5 * pre_act * (1.0 + tanh_val)


def gelu_slope(pre_act):
    square = (3.0 * GELU_CUBIC * pre_act) * pre_act
    tanh_val = jnp.tanh(pre_act * (GELU_SCALE + (GELU_SCALE / 3.0) * square))
    upper = 0.5 + 0.5 * tanh_val
    return upper + ((upper * (1.0 - upper)) * (2.0 * GELU_SCALE * pre_act)) * (1.0 + square)


def activate(pre_act):
    return gelu_value(pre_act.astype(jnp.float32)).astype(jnp.bfloat16)


def back_gate(grad_act, pre_act):
    return (grad_act.astype(jnp.float32) * gelu_slope(pre_act.astype(jnp.float32))).astype(jnp.bfloat16)


def matmul(left_mat, right_mat):
    return jnp.dot(left_mat, right_mat, preferred_element_type=jnp.float32)


def matmul_tn(left_mat, right_mat):
    return lax.dot_general(left_mat, right_mat, TN_DIMS, preferred_element_type=jnp.float32)


def matmul_nt(left_mat, right_mat):
    return lax.dot_general(left_mat, right_mat, NT_DIMS, preferred_element_type=jnp.float32)


def exact_dot(left_mat, right_mat):
    return jnp.dot(left_mat, right_mat, precision=EXACT, preferred_element_type=jnp.float32)


def exact_tn(left_mat, right_mat):
    return lax.dot_general(left_mat, right_mat, TN_DIMS, precision=EXACT, preferred_element_type=jnp.float32)


def reorder(mat, half):
    picks = [jnp.where(half == 0, zero, one) * SUB for zero, one in zip(*LOCAL_ORDER)]
    return jnp.concatenate([lax.dynamic_slice_in_dim(mat, pick, SUB, 1) for pick in picks], 1)


def after(value, *earlier):
    return lax.optimization_barrier((value, *earlier))[0]


def full_gram_part(local_mat):
    own_a = local_mat[:, SUB:2 * SUB]
    own_b = local_mat[:, 2 * SUB:3 * SUB]
    return [matmul_tn(own_a, local_mat[:, :3 * SUB]), matmul_tn(own_b, local_mat[:, 2 * SUB:])]


def block_gram_part(own_mat):
    return [matmul_tn(own_mat[:, :SUB], own_mat), matmul_tn(own_mat[:, SUB:], own_mat[:, SUB:])]


def sum_scatter(part):
    return lax.psum_scatter(part, 'data', scatter_dimension=0, tiled=True)


def spread(piece, over_model):
    found = [piece, lax.ppermute(piece, 'data', CHIP_SWAP)]
    if over_model:
        found += [lax.ppermute(mat, 'model', MODEL_SWAP) for mat in found]
    relayed = [lax.ppermute(mat, 'data', CORE_SWAP) for mat in found]
    return [mat for pair in zip(found, relayed) for mat in pair]


def blend_body(new_scale, blocks, groups, half_tab, piece_tab, flip_tab, place, old_ref, *rest):
    piece_refs, out_ref = rest[:4 * groups], rest[-1]
    entry = pl.program_id(0) * blocks + pl.program_id(1)
    flip = flip_tab[entry]
    distance = lax.bitwise_xor(half_tab[entry], place[0]) if groups == 2 else 0
    part = SUB // 4

    def write(refs, flipped):
        for index, ref in enumerate(refs):
            spot = pl.ds(pl.multiple_of(lax.bitwise_xor(place[1], index) * part, part), part)
            if flipped:
                out_ref[0, :, spot] = FACTOR_DECAY * old_ref[0, :, spot] + new_scale * ref[...].T
            else:
                out_ref[0, spot, :] = FACTOR_DECAY * old_ref[0, spot, :] + new_scale * ref[...]

    for group in range(groups):
        for flipped in (0, 1):
            @pl.when(jnp.logical_and(flip == flipped, distance == group))
            def _():
                write(piece_refs[4 * group:4 * group + 4], flipped)


def blend_layer(old_mats, pieces, first_piece, layer, new_scale, place, partial_out):
    size = old_mats.shape[1]
    blocks = size // SUB
    groups = len(pieces) // 4
    table = FULL_TABLE if blocks == 4 else BLOCK_TABLE
    tables = [jnp.array(column, jnp.int32) for column in zip(*table)] + [place]
    spot = pl.BlockSpec((1, SUB, SUB), lambda row, col, *tabs: (layer, row, col))

    def picked(group):
        def index_map(row, col, halves, names, flips, where):
            entry = row * blocks + col
            needed = lax.bitwise_xor(halves[entry], where[0]) == group if groups == 2 else True
            return 0, first_piece + jnp.where(needed, names[entry], 0)

        return pl.BlockSpec((SUB // 4, SUB), index_map)

    in_specs = [spot] + [picked(index // 4) for index in range(len(pieces))]
    args = [old_mats, *pieces]
    aliases = {}
    if partial_out is not None:
        in_specs.append(pl.BlockSpec(memory_space=pl.ANY))
        args.append(partial_out)
        aliases = {len(tables) + len(args) - 1: 0}
    return pl.pallas_call(
        functools.partial(blend_body, new_scale, blocks, groups),
        grid_spec=pltpu.PrefetchScalarGridSpec(num_scalar_prefetch=len(tables), grid=(blocks, blocks), in_specs=in_specs, out_specs=spot),
        out_shape=jax.ShapeDtypeStruct(old_mats.shape, jnp.float32),
        input_output_aliases=aliases,
        cost_estimate=pl.CostEstimate(flops=3 * size * size, bytes_accessed=12 * size * size, transcendentals=0),
        name='blend_layer',
    )(*tables, *args)


def join_body(place, share_ref, other_ref, *rest):
    out_ref = rest[-1]
    from_share = lax.rem(place[1], 2) == pl.program_id(1)

    @pl.when(from_share)
    def _():
        out_ref[0] = share_ref[...]

    @pl.when(jnp.logical_not(from_share))
    def _():
        out_ref[0] = other_ref[...]


def join_layer(share, other, layer, is_col, place, partial_out):
    rows, cols = share.shape
    step = rows // 4
    shape = (2, 2 * rows, cols) if is_col else (2, rows, 2 * cols)
    taken = pl.BlockSpec((step, cols), lambda row, side, place: (row, 0))
    put = pl.BlockSpec((1, step, cols), lambda row, side, place: (layer, row + 4 * side, 0) if is_col else (layer, row, side))
    in_specs = [taken, taken]
    args = [share, other]
    aliases = {}
    if partial_out is not None:
        in_specs.append(pl.BlockSpec(memory_space=pl.ANY))
        args.append(partial_out)
        aliases = {3: 0}
    return pl.pallas_call(
        join_body,
        grid_spec=pltpu.PrefetchScalarGridSpec(num_scalar_prefetch=1, grid=(4, 2), in_specs=in_specs, out_specs=put),
        out_shape=jax.ShapeDtypeStruct(shape, jnp.float32),
        input_output_aliases=aliases,
        cost_estimate=pl.CostEstimate(flops=2 * rows * cols, bytes_accessed=16 * rows * cols, transcendentals=0),
        name='join_layer',
    )(place, *args)


def solution(mesh):
    data_ways = mesh.shape['data']

    def shard_body(x_tokens, dy_tokens, w_col, w_row, a_old_col, s_old_col, a_old_row, s_old_row, a_inv_col, s_inv_col, a_inv_row, s_inv_row):
        half = lax.axis_index('model')
        quarter = lax.axis_index('data')
        core = lax.rem(quarter, 2)
        inv_rows = 1.0 / (x_tokens.shape[0] * data_ways)
        sent_piece = jnp.where(core == 0, 1 - half, half) * SUB

        place = jnp.stack([half, quarter]).astype(jnp.int32)

        def weight_piece(stack, layer, axis):
            sizes = [1, *stack.shape[1:]]
            sizes[axis + 1] = SUB
            starts = [layer, 0, 0]
            starts[axis + 1] = sent_piece
            return lax.ppermute(lax.dynamic_slice(stack, starts, sizes)[0], 'model', MODEL_SWAP)

        def whole_weight(own, direct, axis):
            relayed = lax.ppermute(direct, 'data', CORE_SWAP)
            low = jnp.where(core == 0, direct, relayed)
            high = jnp.where(core == 0, relayed, direct)
            return jnp.concatenate([low, own, high], axis)

        order = [lax.bitwise_xor(quarter, flip) for flip in (0, 2, 1, 3)]
        mine_at, theirs_at = core * (2 * SUB), (1 - core) * (2 * SUB)
        full_cols, block_cols = 5 * SUB, 3 * SUB

        def wide_product(grad_sum, wide_inv):
            done = exact_dot(grad_sum * inv_rows, wide_inv)
            return done, lax.ppermute(done, 'data', CHIP_SWAP)

        def block_product(pieces, block_inv, is_col, earlier):
            leaving = jnp.concatenate([lax.dynamic_slice_in_dim(mat, theirs_at, 2 * SUB, 1) for mat in pieces], 0)
            staying = [lax.dynamic_slice_in_dim(mat, mine_at, 2 * SUB, 1) for mat in pieces]
            joined = jnp.concatenate(staying + [lax.ppermute(leaving, 'data', CORE_SWAP)], 0)
            rows = block_inv.shape[0] // data_ways
            block_inv = jnp.concatenate([lax.dynamic_slice_in_dim(block_inv, spot * rows, rows, 0) for spot in order], 0)
            joined = after(joined, earlier)
            share = exact_tn(joined, block_inv) if is_col else exact_tn(block_inv, joined)
            return share, lax.ppermute(share, 'data', CORE_SWAP)

        piece_one = weight_piece(w_col, 0, 1)
        piece_two = weight_piece(w_row, 0, 0)
        piece_three = weight_piece(w_col, 1, 1)
        piece_four = weight_piece(w_row, 1, 0)
        weight_one = whole_weight(w_col[0], piece_one, 1)

        edge_part = jnp.concatenate(full_gram_part(reorder(x_tokens, half)) + full_gram_part(reorder(dy_tokens, half)), 1)
        edge_sum = sum_scatter(edge_part)
        edge_all = spread(edge_sum, True)

        z_one = matmul(after(x_tokens, edge_part), weight_one).astype(jnp.bfloat16)
        h_one = activate(z_one)
        h_one_own = h_one[:, OWN]
        weight_two = whole_weight(w_row[0], after(piece_two, h_one), 0)
        early_part = jnp.concatenate(block_gram_part(h_one_own), 1)
        z_two = matmul(after(h_one, early_part, edge_sum), weight_two).astype(jnp.bfloat16)
        h_two = activate(z_two)
        weight_three = whole_weight(w_col[1], after(piece_three, h_two), 1)
        early_part = jnp.concatenate([early_part] + full_gram_part(reorder(h_two, half)), 1)
        early_sum = sum_scatter(early_part)
        z_three = matmul(after(h_two, early_part), weight_three).astype(jnp.bfloat16)
        weight_four = whole_weight(w_row[1], after(piece_four, z_three), 0)
        h_three_own = activate(z_three[:, OWN])
        dw_four_part = matmul_tn(h_three_own, dy_tokens)
        dw_four = sum_scatter(dw_four_part)
        g_three = back_gate(matmul_nt(after(dy_tokens, dw_four_part, edge_all[2]), weight_four).astype(jnp.bfloat16), z_three)
        g_three = after(g_three, early_sum, edge_all[4], edge_all[6])
        h_two_all = spread(early_sum[:, block_cols:], True)
        g_three_own = g_three[:, OWN]
        dw_three_part = matmul_tn(g_three_own, h_two)
        dw_three = sum_scatter(dw_three_part)
        middle_part = jnp.concatenate(block_gram_part(h_three_own) + block_gram_part(g_three_own), 1)
        middle_sum = sum_scatter(middle_part)
        done_four = wide_product(after(dw_four, middle_part), s_inv_row[1])
        g_two = back_gate(matmul_nt(after(g_three, dw_three_part, done_four[0]), weight_three).astype(jnp.bfloat16), z_two)
        dw_two_part = matmul_tn(h_one_own, g_two)
        dw_two = sum_scatter(dw_two_part)
        done_three = wide_product(after(dw_three, dw_two_part), a_inv_col[1])
        g_one_own = back_gate(matmul_nt(after(g_two, done_three[0], h_two_all[2]), w_row[0]).astype(jnp.bfloat16), z_one[:, OWN])
        dw_one_part = matmul_tn(g_one_own, x_tokens)
        dw_one = sum_scatter(dw_one_part)
        g_two_late = after(g_two, dw_one_part, middle_sum, done_four[1])
        mid_all = spread(middle_sum, False)
        late_part = jnp.concatenate(full_gram_part(reorder(g_two_late, half)) + block_gram_part(g_one_own), 1)
        late_sum = sum_scatter(late_part)

        new_scale = (1.0 - FACTOR_DECAY) * inv_rows

        done_two = wide_product(after(dw_two, late_part), s_inv_row[0])
        row_four = block_product(done_four, a_inv_row[1], False, done_two[0])
        spot = after(place, row_four[0])
        a_new_col = blend_layer(a_old_col, edge_all, 0, 0, new_scale, spot, None)
        s_new_row = blend_layer(s_old_row, edge_all, 5, 1, new_scale, spot, None)
        col_three = block_product(done_three, s_inv_col[1], True, after(place, a_new_col, s_new_row))
        done_one = wide_product(after(dw_one, col_three[0], a_new_col, s_new_row), a_inv_col[0])
        spot = after(place, done_one[0])
        a_new_col = blend_layer(a_old_col, h_two_all, 0, 1, new_scale, spot, a_new_col)
        a_new_row = blend_layer(a_old_row, mid_all, 0, 1, new_scale, spot, None)
        s_new_col = blend_layer(s_old_col, mid_all, 3, 1, new_scale, spot, None)
        u_row = join_layer(*row_four, 1, False, spot, None)
        u_col = join_layer(*col_three, 1, True, spot, None)
        outer_all = spread(jnp.concatenate([early_sum[:, :block_cols], late_sum[:, full_cols:]], 1), False)
        g_two_all = spread(late_sum[:, :full_cols], True)
        row_two = block_product(done_two, a_inv_row[0], False, after(place, a_new_col, u_row, u_col, late_sum))
        col_one = block_product(done_one, s_inv_col[0], True, row_two[0])
        spot = after(place, col_one[0])
        u_row = join_layer(*row_two, 0, False, spot, u_row)
        a_new_row = blend_layer(a_old_row, outer_all, 0, 0, new_scale, spot, a_new_row)
        s_new_col = blend_layer(s_old_col, outer_all, 3, 0, new_scale, spot, s_new_col)
        u_col = join_layer(*col_one, 0, True, after(spot, u_row), u_col)
        s_new_row = blend_layer(s_old_row, g_two_all, 0, 0, new_scale, after(spot, u_col), s_new_row)
        return (u_col, u_row, a_new_col, s_new_col, a_new_row, s_new_row)

    batch_split = P('data', None)
    col_split = P(None, None, 'model')
    row_split = P(None, 'model', None)
    replicated = P()
    return jax.shard_map(
        shard_body,
        mesh=mesh,
        in_specs=(batch_split, batch_split, col_split, row_split, replicated, row_split, row_split, replicated, replicated, row_split, row_split, replicated),
        out_specs=(col_split, row_split, replicated, row_split, row_split, replicated),
        check_vma=False,
    )
```

time: 4510 us -> 1480 us (0.33)
  blocking collectives: 1510 us -> 0 us
  waiting for transfers between devices: 1900 us -> 430 us
  matrix products: 926 us -> 656 us
  Pallas kernels: 0 us -> 161 us
  local copies, waits for them, and re-layouts: 12.6 us -> 122 us
  other arithmetic: 137 us -> 53.8 us
    psum x1 -> x0, waiting for transfers between devices: 1900 us -> none  [shard_body(): totals = lax.psum(local_sums, 'data')]
    psum x2 -> x0, blocking collectives: 1510 us -> none  [the longest x1 761 us: local_pass(): z_two = lax.psum(matmul(h_one, w_row[0]), 'model').astype(jnp.bfloat16)]
    ppermute x0 -> x47, waiting for transfers between devices: none -> 430 us  [the longest x5 182 us: spread(): found = [piece, lax.ppermute(piece, 'data', CHIP_SWAP)]]
    dot_general x8 -> x4, matrix products: 418 us -> 74.1 us  [exact_dot(): jnp.dot(left_mat, right_mat, precision=EXACT, preferred_element_type=jnp....]
    pallas_call x0 -> x12, Pallas kernels: none -> 161 us  [the longest x8 118 us: blend_layer(): pl.pallas_call(functools.partial(blend_body, new_scale, blocks, groups),...]
    dot_general x12 -> x20, matrix products: 349 us -> 216 us  [matmul_tn(): lax.dot_general(left_mat, right_mat, TN_DIMS, preferred_element_type=jnp....]
    add x2 -> x0, other arithmetic: 81.3 us -> none  [blend_factor(): FACTOR_DECAY * old_mats]
    dot_general x3, matrix products: 68.8 us -> 147 us  [matmul(): return jnp.dot(left_mat, right_mat, preferred_element_type=jnp.float32)]
  transfers between devices with their start and end apart: 1 -> 55, of which waited for: 1 -> 14; matrix products, arithmetic and copies ran while one was open for 0% -> 44% of each run, Pallas kernels for 0% -> 9%
where the time goes in v2:
time: 1480 us; the launch traced here: 1470 us
  matrix products  656 us (44%)
  waiting for transfers between devices  430 us (29%)
  Pallas kernels  161 us (11%)
  local copies, waits for them, and re-layouts  122 us (8%)
  other arithmetic  53.8 us (4%)
  starting transfers between devices  27.5 us (2%)
  between operations  15.3 us (1%)
    dot_general x20, matrix products, matmul_tn(): lax.dot_general(left_mat, right_mat, TN_DIMS, preferred_element_type=jnp....  216 us
    ppermute x5, waiting for transfers between devices, spread(): found = [piece, lax.ppermute(piece, 'data', CHIP_SWAP)]  182 us
    dot_general x3, matrix products, matmul_nt(): lax.dot_general(left_mat, right_mat, NT_DIMS, preferred_element_type=jnp....  156 us
    dot_general x3, matrix products, matmul(): return jnp.dot(left_mat, right_mat, preferred_element_type=jnp.float32)  147 us
    pallas_call x8, Pallas kernels, blend_layer(): pl.pallas_call(functools.partial(blend_body, new_scale, blocks, groups),...  118 us
    ppermute x4, waiting for transfers between devices, weight_piece(): lax.ppermute(lax.dynamic_slice(stack, starts, sizes)[0], 'model', MODEL_S...  92.8 us
    ppermute x4, waiting for transfers between devices, wide_product(): return (done, lax.ppermute(done, 'data', CHIP_SWAP))  90.8 us
    dot_general x4, matrix products, exact_dot(): jnp.dot(left_mat, right_mat, precision=EXACT, preferred_element_type=jnp....  74.1 us
  transfers between devices with their start and end apart: 55, of which 14 were waited for; matrix products, arithmetic and copies ran while one was open for 44% of the time, Pallas kernels for 9%

profile of v2, /device:TPU:0, one launch (start us, length us, event | category | flops | bytes accessed | tf_op | source)
XLA Modules:
  0.0 1465.6 jit_solution(18305817177138001270)
XLA Ops:
  7.2 22.8 %constant_dynamic-slice_fusion.26 = (bf16[4096,512]{1,0:T(8,128)(2,1)S(1)}, bf16[4096,512]{1,0:T(8,128)(2,1)}, bf16[4096,512]{1,0:T(8,128)(2,1)}, bf16[4096,512]...) fusion(bf16[4096,2048]{1,0:T(8,128)(2,1)} %param.37, ...), kind=kLoop, calls=%fused_computation.279 | loop fusion | bytes 67108880 | tf_op jit(solution)/shard_map/dynamic_slice | solution.py:71
  30.1 10.5 fusion.84
  40.6 11.3 fusion.60
  51.9 10.5 fusion.88
  62.3 11.7 fusion.66
  74.0 7.5 pad_maximum_fusion
  89.0 45.6 %collective-permute-done = bf16[2048,512]{1,0:T(8,128)(2,1)S(1)} collective-permute-done((bf16[2048,512]{1,0:T(8,128)(2,1)S(1)}, bf16[2048,512]{1,0:T(8,128)(2,1)S(1)}, u32[]{:S(2)}, u32[]{:S(2)}) %collective-permute-start) | collective-permute-done | bytes 2097184 | tf_op jit(solution)/shard_map/ppermute | solution.py:208
  134.6 5.1 dynamic-slice_bitcast_fusion
  147.5 53.2 %fusion.17 = (bf16[4096,2048]{1,0:T(8,128)(2,1)}, bf16[4096,2048]{1,0:T(8,128)(2,1)}) fusion(bf16[4096,2048]{1,0:T(8,128)(2,1)} %param.36, bf16[2048,512]{1,0:T(8,128)(2,1)} %get-tuple-element.101, bf16[2048,1024]{1,0:T(8,128)(2,1)} %get-tuple-element.75, bf16[2048,512]{1,0:T(8,128)(2,1)} %get-tuple-element.100), kind=kOutput, calls=%fused_computation.35 | convolution fusion | flops 34468790272 | bytes 58720256 | tf_op jit(solution)/shard_map/dot_general | solution.py:50
  200.7 7.5 slice_bitcast_fusion
  214.2 5.8 fusion.117
  222.6 52.6 %fusion.25 = (bf16[4096,2048]{1,0:T(8,128)(2,1)}, bf16[4096,2048]{1,0:T(8,128)(2,1)}) fusion(bf16[4096,2048]{1,0:T(8,128)(2,1)} %get-tuple-element.29, bf16[512,2048]{1,0:T(8,128)(2,1)} %get-tuple-element.99, bf16[1024,2048]{1,0:T(8,128)(2,1)} %get-tuple-element.71, bf16[512,2048]{1,0:T(8,128)(2,1)} %get-tuple-element.98), kind=kOutput, calls=%fused_computation.43 | convolution fusion | flops 34468790272 | bytes 58720256 | tf_op jit(solution)/shard_map/dot_general | solution.py:50
  275.2 8.7 constant_dynamic-slice_fusion.22
  283.9 5.8 fusion.102
  289.7 12.0 fusion.72
  301.8 5.9 pad_maximum_fusion.1
  309.6 47.2 %collective-permute-done.4 = bf16[2048,512]{1,0:T(8,128)(2,1)S(1)} collective-permute-done((bf16[2048,512]{1,0:T(8,128)(2,1)S(1)}, bf16[2048,512]{1,0:T(8,128)(2,1)S(1)}, u32[]{:S(2)}, u32[]{:S(2)}) %collective-permute-start.4) | collective-permute-done | bytes 2097184 | tf_op jit(solution)/shard_map/ppermute | solution.py:208
  361.2 41.2 %convolution_convert_fusion = bf16[4096,2048]{1,0:T(8,128)(2,1)} fusion(bf16[4096,2048]{1,0:T(8,128)(2,1)} %get-tuple-element.31, bf16[2048,512]{1,0:T(8,128)(2,1)S(1)} %get-tuple-element.97, bf16[2048,1024]{1,0:T(8,128)(2,1)S(1)} %copy-done.13, bf16[2048,512]{1,0:T(8,128)(2,1)S(1)} %get-tuple-element.96), kind=kOutput, calls=%fused_computation.87 | convolution fusion | flops 34393292800 | bytes 41943040 | tf_op jit(solution)/shard_map/dot_general | solution.py:50
  402.4 29.9 %fusion.198 = f32[1024,2048]{1,0:T(8,128)} fusion(bf16[4096,2048]{1,0:T(8,128)(2,1)} %param.37, bf16[4096,2048]{1,0:T(8,128)(2,1)} %convolution_convert_fusion), kind=kOutput, calls=%fused_computation.307 | convolution fusion | flops 17217617920 | bytes 33554432 | tf_op jit(solution)/shard_map/dot_general | solution.py:54
  436.0 98.1 %collective-permute-done.6.rest_2_ = f32[128,5120]{1,0:T(8,128)} collective-permute-done((f32[128,5120]{1,0:T(8,128)S(1)}, f32[128,5120]{1,0:T(8,128)}, u32[]{:S(2)}, u32[]{:S(2)}) %collective-permute-start.6) | collective-permute-done | bytes 2621472 | tf_op jit(solution)/shard_map/ppermute | solution.py:93
  537.9 62.8 %fusion.13 = bf16[4096,2048]{1,0:T(8,128)(2,1)} fusion(bf16[4096,2048]{1,0:T(8,128)(2,1)} %convolution_convert_fusion, bf16[4096,2048]{1,0:T(8,128)(2,1)} %param.37, bf16[512,2048]{1,0:T(8,128)(2,1)} %get-tuple-element.95, bf16[1024,2048]{1,0:T(8,128)(2,1)} %get-tuple-element.70, bf16[512,2048]{1,0:T(8,128)(2,1)} %get-tuple-element.94), kind=kOutput, calls=%fused_computation.31 | convolution fusion | flops 34544287744 | bytes 58720256 | tf_op jit(solution)/shard_map/dot_general | solution.py:58
  600.8 24.6 %fusion.121 = f32[1024,2048]{1,0:T(8,128)} fusion(bf16[4096,2048]{1,0:T(8,128)(2,1)} %fusion.13, bf16[4096,2048]{1,0:T(8,128)(2,1)} %get-tuple-element.121), kind=kOutput, calls=%fused_computation.155 | convolution fusion | flops 17255366656 | bytes 33554432 | tf_op jit(solution)/shard_map/dot_general | solution.py:54
  625.5 7.8 fusion.41
  652.2 18.8 %fusion.54 = f32[256,2048]{1,0:T(8,128)} fusion(f32[2,2048,2048]{2,1,0:T(8,128)} %param.47, f32[256,2048]{1,0:T(8,128)} %reduce-scatter.13.cloned.1.call-done), kind=kOutput, calls=%fused_computation.81 | convolution fusion | flops 12885426176 | bytes 20971520 | tf_op jit(solution)/shard_map/dot_general | solution.py:62
  671.1 62.4 %fusion.8 = bf16[4096,2048]{1,0:T(8,128)(2,1)} fusion(bf16[4096,2048]{1,0:T(8,128)(2,1)} %get-tuple-element.121, bf16[4096,2048]{1,0:T(8,128)(2,1)} %fusion.13, bf16[2048,512]{1,0:T(8,128)(2,1)} %copy-done.22, bf16[2048,1024]{1,0:T(8,128)(2,1)} %get-tuple-element.74, bf16[2048,512]{1,0:T(8,128)(2,1)S(1)} %copy-done.21), kind=kOutput, calls=%fused_computation.26 | convolution fusion | flops 34544287744 | bytes 58720256 | tf_op jit(solution)/shard_map/dot_general | solution.py:58
  733.5 24.1 %fusion.115 = f32[1024,2048]{1,0:T(8,128)} fusion(bf16[4096,2048]{1,0:T(8,128)(2,1)} %fusion.8, bf16[4096,2048]{1,0:T(8,128)(2,1)} %get-tuple-element.29), kind=kOutput, calls=%fused_computation.149 | convolution fusion | flops 17179869184 | bytes 33554432 | tf_op jit(solution)/shard_map/dot_general | solution.py:54
  761.4 19.3 %fusion.52 = f32[256,2048]{1,0:T(8,128)} fusion(f32[2,2048,2048]{2,1,0:T(8,128)} %param.44, f32[256,2048]{1,0:T(8,128)} %reduce-scatter.15.cloned.1.call-done), kind=kOutput, calls=%fused_computation.79 | convolution fusion | flops 12885426176 | bytes 20971520 | tf_op jit(solution)/shard_map/dot_general | solution.py:62
  780.7 20.6 %collective-permute-done.11.rest_2_ = f32[128,2560]{1,0:T(8,128)S(1)} collective-permute-done((f32[128,2560]{1,0:T(8,128)S(1)}, f32[128,2560]{1,0:T(8,128)S(1)}, u32[]{:S(2)}, u32[]{:S(2)}) %collective-permute-start.11) | collective-permute-done | bytes 1310752 | tf_op jit(solution)/shard_map/ppermute | solution.py:93
  801.2 30.9 %fusion.38 = bf16[4096,1024]{1,0:T(8,128)(2,1)S(1)} fusion(bf16[4096,2048]{1,0:T(8,128)(2,1)} %get-tuple-element.119, bf16[4096,2048]{1,0:T(8,128)(2,1)} %fusion.8, bf16[2,1024,2048]{2,1,0:T(8,128)(2,1)} %param.39), kind=kOutput, calls=%fused_computation.65 | convolution fusion | flops 17259560960 | bytes 37748736 | tf_op jit(solution)/shard_map/dot_general | solution.py:58
  835.5 21.8 %fusion.203 = f32[1024,2048]{1,0:T(8,128)} fusion(bf16[4096,1024]{1,0:T(8,128)(2,1)S(1)} %fusion.38, bf16[4096,2048]{1,0:T(8,128)(2,1)} %param.36), kind=kOutput, calls=%fused_computation.310 | convolution fusion | flops 17179869184 | bytes 33554432 | tf_op jit(solution)/shard_map/dot_general | solution.py:54
  861.4 66.7 %collective-permute-done.14 = f32[256,2048]{1,0:T(8,128)} collective-permute-done((f32[256,2048]{1,0:T(8,128)S(1)}, f32[256,2048]{1,0:T(8,128)}, u32[]{:S(2)}, u32[]{:S(2)}) %collective-permute-start.14) | collective-permute-done | bytes 2097184 | tf_op jit(solution)/shard_map/ppermute | solution.py:222
  928.1 5.8 fusion.123
  934.0 8.6 constant_dynamic-slice_fusion.10
  947.1 10.5 fusion.125
  957.6 11.5 fusion.78
  969.1 5.6 pad_maximum_fusion.3
  983.0 6.1 fusion.201
  992.9 7.0 fusion.202
  1000.5 11.2 collective-permute-done.12
  1027.4 18.7 %fusion.50 = f32[256,2048]{1,0:T(8,128)} fusion(f32[2,2048,2048]{2,1,0:T(8,128)} %param.47, f32[256,2048]{1,0:T(8,128)} %reduce-scatter.19.cloned.1.call-done), kind=kOutput, calls=%fused_computation.77 | convolution fusion | flops 12885426176 | bytes 20971520 | tf_op jit(solution)/shard_map/dot_general | solution.py:62
  1048.6 15.4 %fusion.142.share_ref = f32[1024,1024]{1,0:T(8,128)} fusion(f32[1024,1024]{1,0:T(8,128)S(1)} %copy-done.12, f32[256,1024]{1,0:T(8,128)S(1)} %copy-done.38, f32[256,1024]{1,0:T(8,128)S(1)} %copy-done.37, f32[256,1024]{1,0:T(8,128)S(1)} %copy-done.36, f32[256,1024]{1,0:T(8,128)S(1)} %copy-done.39), kind=kOutput, calls=%fused_computation.178 | convolution fusion | flops 12888047616 | bytes 12582912 | tf_op jit(solution)/shard_map/dot_general | solution.py:66
  1066.2 23.3 %blend_layer.9.rest_8_ = f32[2,2048,2048]{2,1,0:T(8,128)} custom-call(s32[16]{0:T(128)} %constant.78.clone.half_tab, s32[16]{0:T(128)} %constant.79.clone.piece_tab, s32[16]{0:T(128)} %constant.80.clone.flip_tab, s32[2]{0:T(128)} %pad_add_fusion.place, f32[2,2048,2048]{2,1,0:T(8,128)} %old_ref.15, f32[128,5120]{1,0:T(8,128)} %reduce-scatter.9.cloned.1.call-done.rest_0_, ...), custom_call_target="tpu_custom_call" | custom-call | flops 12582912 | bytes 50331648 | tf_op jit(solution)/shard_map/blend_layer/pallas_call | solution.py:145
  1089.5 23.4 %blend_layer.8.rest_8_ = f32[2,2048,2048]{2,1,0:T(8,128)} custom-call(s32[16]{0:T(128)} %constant.78.clone.half_tab, s32[16]{0:T(128)} %constant.79.clone.piece_tab, s32[16]{0:T(128)} %constant.80.clone.flip_tab, s32[2]{0:T(128)} %pad_add_fusion.place, f32[2,2048,2048]{2,1,0:T(8,128)} %old_ref.10, f32[128,5120]{1,0:T(8,128)} %reduce-scatter.9.cloned.1.call-done.rest_0_, ...), custom_call_target="tpu_custom_call" | custom-call | flops 12582912 | bytes 50331648 | tf_op jit(solution)/shard_map/blend_layer/pallas_call | solution.py:145
  1115.7 15.0 %fusion.134.share_ref = f32[1024,1024]{1,0:T(8,128)} fusion(f32[1024,1024]{1,0:T(8,128)S(1)} %pad_maximum_fusion.5, f32[256,1024]{1,0:T(8,128)S(1)} %copy-done.33, f32[256,1024]{1,0:T(8,128)S(1)} %copy-done.34, f32[256,1024]{1,0:T(8,128)S(1)} %copy-done.35, f32[256,1024]{1,0:T(8,128)S(1)} %copy-done.32), kind=kOutput, calls=%fused_computation.170 | convolution fusion | flops 12888047616 | bytes 12582912 | tf_op jit(solution)/shard_map/dot_general | solution.py:66
  1130.8 17.3 %fusion.48 = f32[256,2048]{1,0:T(8,128)S(1)} fusion(f32[2,2048,2048]{2,1,0:T(8,128)} %param.44, f32[256,2048]{1,0:T(8,128)} %reduce-scatter.17.cloned.1.call-done), kind=kOutput, calls=%fused_computation.75 | convolution fusion | flops 12885426176 | bytes 20971520 | tf_op jit(solution)/shard_map/dot_general | solution.py:62
  1154.2 29.0 %collective-permute-done.32.rest_6_ = f32[128,2560]{1,0:T(8,128)S(1)} collective-permute-done((f32[128,2560]{1,0:T(8,128)S(1)}, f32[128,2560]{1,0:T(8,128)S(1)}, u32[]{:S(2)}, u32[]{:S(2)}) %collective-permute-start.32) | collective-permute-done | bytes 1310752 | tf_op jit(solution)/shard_map/ppermute | solution.py:95
  1183.2 12.9 collective-permute-done.20
  1200.1 15.0 %fusion.150.share_ref = f32[1024,1024]{1,0:T(8,128)} fusion(f32[1024,1024]{1,0:T(8,128)S(1)} %pad_maximum_fusion.8, f32[256,1024]{1,0:T(8,128)S(1)} %get-tuple-element.83, f32[256,1024]{1,0:T(8,128)S(1)} %get-tuple-element.84, f32[256,1024]{1,0:T(8,128)S(1)} %get-tuple-element.85, f32[256,1024]{1,0:T(8,128)S(1)} %get-tuple-element.82), kind=kOutput, calls=%fused_computation.188 | convolution fusion | flops 12888047616 | bytes 12582912 | tf_op jit(solution)/shard_map/dot_general | solution.py:66
  1215.6 18.6 %collective-permute-done.38.rest_2_ = f32[128,3072]{1,0:T(8,128)} collective-permute-done((f32[128,3072]{1,0:T(8,128)S(1)}, f32[128,3072]{1,0:T(8,128)}, u32[]{:S(2)}, u32[]{:S(2)}) %collective-permute-start.38) | collective-permute-done | bytes 1572896 | tf_op jit(solution)/shard_map/ppermute | solution.py:93
  1243.9 16.8 %fusion.158.share_ref = f32[1024,1024]{1,0:T(8,128)} fusion(f32[1024,1024]{1,0:T(8,128)S(1)} %pad_maximum_fusion.7, f32[256,1024]{1,0:T(8,128)} %get-tuple-element.79, f32[256,1024]{1,0:T(8,128)} %get-tuple-element.80, f32[256,1024]{1,0:T(8,128)} %get-tuple-element.81, f32[256,1024]{1,0:T(8,128)} %get-tuple-element.78), kind=kOutput, calls=%fused_computation.197 | convolution fusion | flops 12888047616 | bytes 12582912 | tf_op jit(solution)/shard_map/dot_general | solution.py:66
  1263.9 17.0 %collective-permute-done.35.rest_2_ = f32[128,3072]{1,0:T(8,128)S(1)} collective-permute-done((f32[128,3072]{1,0:T(8,128)S(1)}, f32[128,3072]{1,0:T(8,128)S(1)}, u32[]{:S(2)}, u32[]{:S(2)}) %collective-permute-start.35) | collective-permute-done | bytes 1572896 | tf_op jit(solution)/shard_map/ppermute | solution.py:93
  1281.0 27.2 %collective-permute-done.41.rest_2_ = f32[128,2560]{1,0:T(8,128)} collective-permute-done((f32[128,2560]{1,0:T(8,128)}, f32[128,2560]{1,0:T(8,128)}, u32[]{:S(2)}, u32[]{:S(2)}) %collective-permute-start.41) | collective-permute-done | bytes 1310752 | tf_op jit(solution)/shard_map/ppermute | solution.py:93
  1308.2 4.8 collective-permute-done.43.rest_4_
  1313.4 27.1 %collective-permute-done.45.rest_6_ = f32[128,2560]{1,0:T(8,128)} collective-permute-done((f32[128,2560]{1,0:T(8,128)}, f32[128,2560]{1,0:T(8,128)}, u32[]{:S(2)}, u32[]{:S(2)}) %collective-permute-start.45) | collective-permute-done | bytes 1310752 | tf_op jit(solution)/shard_map/ppermute | solution.py:95
  1342.2 10.8 join_layer.6.rest_0_
  1353.0 10.8 join_layer.4.rest_0_
  1364.3 6.2 blend_layer.13.rest_4_
  1370.5 6.2 blend_layer.11.rest_4_
  1376.8 23.3 %blend_layer.10 = f32[2,2048,2048]{2,1,0:T(8,128)} custom-call(s32[16]{0:T(128)} %constant.78.clone.half_tab, s32[16]{0:T(128)} %constant.79.clone.piece_tab, s32[16]{0:T(128)} %constant.80.clone.flip_tab, s32[2]{0:T(128)} %pad_add_fusion.place, f32[2,2048,2048]{2,1,0:T(8,128)} %old_ref.10, f32[128,2560]{1,0:T(8,128)} %copy-done.9, ...), custom_call_target="tpu_custom_call", output_to_operand_aliasing={{}: (13, {})} | custom-call | flops 12582912 | bytes 50331648 | tf_op jit(solution)/shard_map/blend_layer/pallas_call | solution.py:145
  1400.0 10.8 join_layer.5
  1410.8 6.2 blend_layer.14
  1417.0 6.2 blend_layer.12
  1423.2 10.8 join_layer.7
  1435.1 23.3 %blend_layer.15 = f32[2,2048,2048]{2,1,0:T(8,128)} custom-call(s32[16]{0:T(128)} %constant.78.clone.half_tab, s32[16]{0:T(128)} %constant.79.clone.piece_tab, s32[16]{0:T(128)} %constant.80.clone.flip_tab, s32[2]{0:T(128)} %pad_add_fusion.place, f32[2,2048,2048]{2,1,0:T(8,128)} %old_ref.15, ...), custom_call_target="tpu_custom_call", output_to_operand_aliasing={{}: (13, {})} | custom-call | flops 12582912 | bytes 50331648 | tf_op jit(solution)/shard_map/blend_layer/pallas_call | solution.py:145
  (242 shorter events, 135.1 us)
Async XLA Ops:
  7.2 215.4 %reduce-scatter.9.cloned.1.call-start = ((), (), s32[]{:S(2)}) async-start(), calls=%async_computation.8 | async-start | bytes 13107200 | tf_op jit(solution)/shard_map/reduce_scatter | solution.py:89
  81.6 519.2 %reduce-scatter.11.cloned.1.call-start = ((), (), s32[]{:S(2)}) async-start(), calls=%async_computation.9 | async-start | bytes 10485760 | tf_op jit(solution)/shard_map/reduce_scatter | solution.py:89
  81.6 59.7 %slice-start = ((s8[8388608]{0:T(1024)(128)(4,1)}), s8[4194304]{0:T(1024)(128)(4,1)S(1)}, s32[]{:S(2)}) async-start(s8[8388608]{0:T(1024)(128)(4,1)} %bitcast.87), calls=%async_computation.16 | async-start | bytes 8388608
  85.6 55.8 %slice-start.1 = ((s8[8388608]{0:T(1024)(128)(4,1)}), s8[4194304]{0:T(1024)(128)(4,1)S(1)}, s32[]{:S(2)}) async-start(s8[8388608]{0:T(1024)(128)(4,1)} %bitcast.87), calls=%async_computation.17 | async-start | bytes 8388608
  85.6 49.0 %collective-permute-start = (bf16[2048,512]{1,0:T(8,128)(2,1)S(1)}, bf16[2048,512]{1,0:T(8,128)(2,1)S(1)}, u32[]{:S(2)}, u32[]{:S(2)}) collective-permute-start(bf16[2048,512]{1,0:T(8,128)(2,1)S(1)} %get-tuple-element.77), channel_id=1, source_target_pairs={{0,4},{4,0},{1,5},{5,1},{2,6},{6,2},{3,7},{7,3}} | collective-permute-start | bytes 6291464 | tf_op jit(solution)/shard_map/ppermute | solution.py:208
  134.6 10.6 collective-permute-start.1
  139.7 61.0 %collective-permute-start.2 = (bf16[512,2048]{1,0:T(8,128)(2,1)}, bf16[512,2048]{1,0:T(8,128)(2,1)S(1)}, u32[]{:S(2)}, u32[]{:S(2)}) collective-permute-start(bf16[512,2048]{1,0:T(8,128)(2,1)} %get-tuple-element.73), channel_id=1, source_target_pairs={{0,4},{4,0},{1,5},{5,1},{2,6},{6,2},{3,7},{7,3}} | collective-permute-start | bytes 6291464 | tf_op jit(solution)/shard_map/ppermute | solution.py:208
  200.7 19.3 %collective-permute-start.3 = (bf16[512,2048]{1,0:T(8,128)(2,1)S(1)}, bf16[512,2048]{1,0:T(8,128)(2,1)S(1)}, u32[]{:S(2)}, u32[]{:S(2)}) collective-permute-start(bf16[512,2048]{1,0:T(8,128)(2,1)S(1)} %collective-permute-done.2), channel_id=1, source_target_pairs={{0,1},{1,0},{2,3},{3,2},{4,5},{5,4},{6,7},{7,6}} | collective-permute-start | bytes 6291464 | tf_op jit(solution)/shard_map/ppermute | solution.py:211
  307.7 344.6 %reduce-scatter.13.cloned.1.call-start = ((), (), s32[]{:S(2)}) async-start(), calls=%async_computation.10 | async-start | bytes 10485760 | tf_op jit(solution)/shard_map/reduce_scatter | solution.py:89
  307.7 53.5 %copy-start.13 = (bf16[2048,1024]{1,0:T(8,128)(2,1)S(1)}, bf16[2048,1024]{1,0:T(8,128)(2,1)}, u32[]{:S(2)}) copy-start(bf16[2048,1024]{1,0:T(8,128)(2,1)} %get-tuple-element.74) | copy-start | bytes 12582916
  309.2 47.5 %collective-permute-start.4 = (bf16[2048,512]{1,0:T(8,128)(2,1)S(1)}, bf16[2048,512]{1,0:T(8,128)(2,1)S(1)}, u32[]{:S(2)}, u32[]{:S(2)}) collective-permute-start(bf16[2048,512]{1,0:T(8,128)(2,1)S(1)} %copy-done.23), channel_id=1, source_target_pairs={{0,4},{4,0},{1,5},{5,1},{2,6},{6,2},{3,7},{7,3}} | collective-permute-start | bytes 6291464 | tf_op jit(solution)/shard_map/ppermute | solution.py:208
  356.8 4.2 collective-permute-start.5
  356.8 78.6 %collective-permute-start.7 = (bf16[512,2048]{1,0:T(8,128)(2,1)}, bf16[512,2048]{1,0:T(8,128)(2,1)}, u32[]{:S(2)}, u32[]{:S(2)}) collective-permute-start(bf16[512,2048]{1,0:T(8,128)(2,1)} %get-tuple-element.72), channel_id=1, source_target_pairs={{0,4},{4,0},{1,5},{5,1},{2,6},{6,2},{3,7},{7,3}} | collective-permute-start | bytes 6291464 | tf_op jit(solution)/shard_map/ppermute | solution.py:208
  361.2 41.2 %copy-start.20 = (bf16[2048,512]{1,0:T(8,128)(2,1)}, bf16[2048,512]{1,0:T(8,128)(2,1)S(1)}, u32[]{:S(2)}) copy-start(bf16[2048,512]{1,0:T(8,128)(2,1)S(1)} %get-tuple-element.96) | copy-start | bytes 6291460
  361.2 41.2 %copy-start.22 = (bf16[2048,512]{1,0:T(8,128)(2,1)}, bf16[2048,512]{1,0:T(8,128)(2,1)S(1)}, u32[]{:S(2)}) copy-start(bf16[2048,512]{1,0:T(8,128)(2,1)S(1)} %get-tuple-element.97) | copy-start | bytes 6291460
  432.3 329.1 %reduce-scatter.15.cloned.1.call-start = ((), (), s32[]{:S(2)}) async-start(), calls=%async_computation.11 | async-start | bytes 10485760 | tf_op jit(solution)/shard_map/reduce_scatter | solution.py:89
  434.0 100.1 %collective-permute-start.6 = (f32[128,5120]{1,0:T(8,128)S(1)}, f32[128,5120]{1,0:T(8,128)}, u32[]{:S(2)}, u32[]{:S(2)}) collective-permute-start(f32[128,5120]{1,0:T(8,128)S(1)} %copy-done.2), channel_id=1, source_target_pairs={{0,2},{2,0},{1,3},{3,1},{4,6},{6,4},{5,7},{7,5}} | collective-permute-start | bytes 7864328 | tf_op jit(solution)/shard_map/ppermute | solution.py:93
  435.4 98.7 %collective-permute-start.8 = (bf16[512,2048]{1,0:T(8,128)(2,1)}, bf16[512,2048]{1,0:T(8,128)(2,1)S(1)}, u32[]{:S(2)}, u32[]{:S(2)}) collective-permute-start(bf16[512,2048]{1,0:T(8,128)(2,1)} %collective-permute-done.7), channel_id=1, source_target_pairs={{0,1},{1,0},{2,3},{3,2},{4,5},{5,4},{6,7},{7,6}} | collective-permute-start | bytes 6291464 | tf_op jit(solution)/shard_map/ppermute | solution.py:211
  435.4 165.3 %collective-permute-start.9 = (f32[128,5120]{1,0:T(8,128)S(1)}, f32[128,5120]{1,0:T(8,128)}, u32[]{:S(2)}, u32[]{:S(2)}) collective-permute-start(f32[128,5120]{1,0:T(8,128)S(1)} %copy-done.2), channel_id=1, source_target_pairs={{0,4},{4,0},{1,5},{5,1},{2,6},{6,2},{3,7},{7,3}} | collective-permute-start | bytes 7864328 | tf_op jit(solution)/shard_map/ppermute | solution.py:95
  534.1 66.6 %collective-permute-start.10 = (f32[128,5120]{1,0:T(8,128)}, f32[128,5120]{1,0:T(8,128)}, u32[]{:S(2)}, u32[]{:S(2)}) collective-permute-start(f32[128,5120]{1,0:T(8,128)} %collective-permute-done.6.rest_2_), channel_id=1, source_target_pairs={{0,4},{4,0},{1,5},{5,1},{2,6},{6,2},{3,7},{7,3}} | collective-permute-start | bytes 7864328 | tf_op jit(solution)/shard_map/ppermute | solution.py:95
  625.4 302.7 %reduce-scatter.21.cloned.1.call-start = ((), (), s32[]{:S(2)}) async-start(), calls=%async_computation.14 | async-start | bytes 7864320 | tf_op jit(solution)/shard_map/reduce_scatter | solution.py:89
  652.2 375.2 %reduce-scatter.19.cloned.1.call-start = ((), (), s32[]{:S(2)}) async-start(), calls=%async_computation.13 | async-start | bytes 10485760 | tf_op jit(solution)/shard_map/reduce_scatter | solution.py:89
  757.6 373.1 %reduce-scatter.17.cloned.1.call-start = ((), (), s32[]{:S(2)}) async-start(), calls=%async_computation.12 | async-start | bytes 10485760 | tf_op jit(solution)/shard_map/reduce_scatter | solution.py:89
  759.3 41.9 %collective-permute-start.11 = (f32[128,2560]{1,0:T(8,128)S(1)}, f32[128,2560]{1,0:T(8,128)S(1)}, u32[]{:S(2)}, u32[]{:S(2)}) collective-permute-start(f32[128,2560]{1,0:T(8,128)S(1)} %slice.143.rest_0_), channel_id=1, source_target_pairs={{0,2},{2,0},{1,3},{3,1},{4,6},{6,4},{5,7},{7,5}} | collective-permute-start | bytes 3932168 | tf_op jit(solution)/shard_map/ppermute | solution.py:93
  801.2 30.9 %copy-start.25 = (f32[128,2560]{1,0:T(8,128)}, f32[128,2560]{1,0:T(8,128)S(1)}, u32[]{:S(2)}) copy-start(f32[128,2560]{1,0:T(8,128)S(1)} %collective-permute-done.11.rest_2_) | copy-start | bytes 3932164
  857.3 380.8 %reduce-scatter.23.cloned.1.call-start = ((), (), s32[]{:S(2)}) async-start(), calls=%async_computation.15 | async-start | bytes 10485760 | tf_op jit(solution)/shard_map/reduce_scatter | solution.py:89
  858.9 69.3 %collective-permute-start.14 = (f32[256,2048]{1,0:T(8,128)S(1)}, f32[256,2048]{1,0:T(8,128)}, u32[]{:S(2)}, u32[]{:S(2)}) collective-permute-start(f32[256,2048]{1,0:T(8,128)S(1)} %copy-done.4), channel_id=1, source_target_pairs={{0,2},{2,0},{1,3},{3,1},{4,6},{6,4},{5,7},{7,5}} | collective-permute-start | bytes 6291464 | tf_op jit(solution)/shard_map/ppermute | solution.py:222
  974.8 36.9 %collective-permute-start.12 = (f32[256,2048]{1,0:T(8,128)}, f32[256,2048]{1,0:T(8,128)}, u32[]{:S(2)}, u32[]{:S(2)}) collective-permute-start(f32[256,2048]{1,0:T(8,128)} %fusion.52), channel_id=1, source_target_pairs={{0,2},{2,0},{1,3},{3,1},{4,6},{6,4},{5,7},{7,5}} | collective-permute-start | bytes 6291464 | tf_op jit(solution)/shard_map/ppermute | solution.py:222
  983.0 35.7 %collective-permute-start.15 = (f32[512,1024]{1,0:T(8,128)}, f32[512,1024]{1,0:T(8,128)}, u32[]{:S(2)}, u32[]{:S(2)}) collective-permute-start(f32[512,1024]{1,0:T(8,128)} %pad_maximum_fusion.12), channel_id=1, source_target_pairs={{0,1},{1,0},{2,3},{3,2},{4,5},{5,4},{6,7},{7,6}} | collective-permute-start | bytes 6291464 | tf_op jit(solution)/shard_map/ppermute | solution.py:227
  992.4 53.8 %collective-permute-start.16 = (f32[128,5120]{1,0:T(8,128)S(1)}, f32[128,5120]{1,0:T(8,128)}, u32[]{:S(2)}, u32[]{:S(2)}) collective-permute-start(f32[128,5120]{1,0:T(8,128)S(1)} %copy-done.3), channel_id=1, source_target_pairs={{0,1},{1,0},{2,3},{3,2},{4,5},{5,4},{6,7},{7,6}} | collective-permute-start | bytes 7864328 | tf_op jit(solution)/shard_map/ppermute | solution.py:96
  999.9 64.1 %collective-permute-start.17 = (f32[128,5120]{1,0:T(8,128)}, f32[128,5120]{1,0:T(8,128)}, u32[]{:S(2)}, u32[]{:S(2)}) collective-permute-start(f32[128,5120]{1,0:T(8,128)} %collective-permute-done.6.rest_2_), channel_id=1, source_target_pairs={{0,1},{1,0},{2,3},{3,2},{4,5},{5,4},{6,7},{7,6}} | collective-permute-start | bytes 7864328 | tf_op jit(solution)/shard_map/ppermute | solution.py:96
  999.9 66.2 %collective-permute-start.18 = (f32[128,5120]{1,0:T(8,128)}, f32[128,5120]{1,0:T(8,128)}, u32[]{:S(2)}, u32[]{:S(2)}) collective-permute-start(f32[128,5120]{1,0:T(8,128)} %collective-permute-done.9.rest_4_), channel_id=1, source_target_pairs={{0,1},{1,0},{2,3},{3,2},{4,5},{5,4},{6,7},{7,6}} | collective-permute-start | bytes 7864328 | tf_op jit(solution)/shard_map/ppermute | solution.py:96
  1011.7 54.5 %collective-permute-start.19 = (f32[128,5120]{1,0:T(8,128)}, f32[128,5120]{1,0:T(8,128)}, u32[]{:S(2)}, u32[]{:S(2)}) collective-permute-start(f32[128,5120]{1,0:T(8,128)} %collective-permute-done.10.rest_6_), channel_id=1, source_target_pairs={{0,1},{1,0},{2,3},{3,2},{4,5},{5,4},{6,7},{7,6}} | collective-permute-start | bytes 7864328 | tf_op jit(solution)/shard_map/ppermute | solution.py:96
  1018.6 94.3 %collective-permute-start.13 = (f32[512,1024]{1,0:T(8,128)}, f32[512,1024]{1,0:T(8,128)}, u32[]{:S(2)}, u32[]{:S(2)}) collective-permute-start(f32[512,1024]{1,0:T(8,128)} %pad_maximum_fusion.11), channel_id=1, source_target_pairs={{0,1},{1,0},{2,3},{3,2},{4,5},{5,4},{6,7},{7,6}} | collective-permute-start | bytes 6291464 | tf_op jit(solution)/shard_map/ppermute | solution.py:227
  1046.2 103.7 %collective-permute-start.22 = (f32[256,2048]{1,0:T(8,128)}, f32[256,2048]{1,0:T(8,128)}, u32[]{:S(2)}, u32[]{:S(2)}) collective-permute-start(f32[256,2048]{1,0:T(8,128)} %fusion.50), channel_id=1, source_target_pairs={{0,2},{2,0},{1,3},{3,1},{4,6},{6,4},{5,7},{7,5}} | collective-permute-start | bytes 6291464 | tf_op jit(solution)/shard_map/ppermute | solution.py:222
  1064.1 88.4 %collective-permute-start.30 = (f32[128,2560]{1,0:T(8,128)S(1)}, f32[128,2560]{1,0:T(8,128)}, u32[]{:S(2)}, u32[]{:S(2)}) collective-permute-start(f32[128,2560]{1,0:T(8,128)S(1)} %copy-done.10), channel_id=1, source_target_pairs={{0,4},{4,0},{1,5},{5,1},{2,6},{6,2},{3,7},{7,3}} | collective-permute-start | bytes 3932168 | tf_op jit(solution)/shard_map/ppermute | solution.py:95
  1066.1 86.4 %collective-permute-start.28 = (f32[128,2560]{1,0:T(8,128)S(1)}, f32[128,2560]{1,0:T(8,128)}, u32[]{:S(2)}, u32[]{:S(2)}) collective-permute-start(f32[128,2560]{1,0:T(8,128)S(1)} %copy-done.10), channel_id=1, source_target_pairs={{0,1},{1,0},{2,3},{3,2},{4,5},{5,4},{6,7},{7,6}} | collective-permute-start | bytes 3932168 | tf_op jit(solution)/shard_map/ppermute | solution.py:96
  1148.0 48.1 %collective-permute-start.20 = (f32[256,2048]{1,0:T(8,128)S(1)}, f32[256,2048]{1,0:T(8,128)S(1)}, u32[]{:S(2)}, u32[]{:S(2)}) collective-permute-start(f32[256,2048]{1,0:T(8,128)S(1)} %fusion.48), channel_id=1, source_target_pairs={{0,2},{2,0},{1,3},{3,1},{4,6},{6,4},{5,7},{7,5}} | collective-permute-start | bytes 6291464 | tf_op jit(solution)/shard_map/ppermute | solution.py:222
  1149.9 47.4 %copy-start.8 = (f32[128,3072]{1,0:T(8,128)S(1)}, f32[128,3072]{1,0:T(8,128)}, u32[]{:S(2)}) copy-start(f32[128,3072]{1,0:T(8,128)} %reduce-scatter.21.cloned.1.call-done.rest_0_) | copy-start | bytes 4718596
  1151.7 47.4 %copy-start = (f32[1,1024,1024]{2,1,0:T(8,128)S(1)}, f32[1,1024,1024]{2,1,0:T(8,128)}, u32[]{:S(2)}) copy-start(f32[1,1024,1024]{2,1,0:T(8,128)} %get-tuple-element.68) | copy-start | bytes 12582916
  1151.9 46.6 %collective-permute-start.23 = (f32[512,1024]{1,0:T(8,128)S(1)}, f32[512,1024]{1,0:T(8,128)S(1)}, u32[]{:S(2)}, u32[]{:S(2)}) collective-permute-start(f32[512,1024]{1,0:T(8,128)S(1)} %pad_maximum_fusion.14), channel_id=1, source_target_pairs={{0,1},{1,0},{2,3},{3,2},{4,5},{5,4},{6,7},{7,6}} | collective-permute-start | bytes 6291464 | tf_op jit(solution)/shard_map/ppermute | solution.py:227
  1152.5 30.7 %collective-permute-start.32 = (f32[128,2560]{1,0:T(8,128)S(1)}, f32[128,2560]{1,0:T(8,128)S(1)}, u32[]{:S(2)}, u32[]{:S(2)}) collective-permute-start(f32[128,2560]{1,0:T(8,128)S(1)} %copy-done.26), channel_id=1, source_target_pairs={{0,4},{4,0},{1,5},{5,1},{2,6},{6,2},{3,7},{7,3}} | collective-permute-start | bytes 3932168 | tf_op jit(solution)/shard_map/ppermute | solution.py:95
  1152.5 44.8 %collective-permute-start.29 = (f32[128,2560]{1,0:T(8,128)S(1)}, f32[128,2560]{1,0:T(8,128)S(1)}, u32[]{:S(2)}, u32[]{:S(2)}) collective-permute-start(f32[128,2560]{1,0:T(8,128)S(1)} %copy-done.26), channel_id=1, source_target_pairs={{0,1},{1,0},{2,3},{3,2},{4,5},{5,4},{6,7},{7,6}} | collective-permute-start | bytes 3932168 | tf_op jit(solution)/shard_map/ppermute | solution.py:96
  1152.6 47.5 %collective-permute-start.31 = (f32[128,2560]{1,0:T(8,128)}, f32[128,2560]{1,0:T(8,128)S(1)}, u32[]{:S(2)}, u32[]{:S(2)}) collective-permute-start(f32[128,2560]{1,0:T(8,128)} %collective-permute-done.30.rest_4_), channel_id=1, source_target_pairs={{0,1},{1,0},{2,3},{3,2},{4,5},{5,4},{6,7},{7,6}} | collective-permute-start | bytes 3932168 | tf_op jit(solution)/shard_map/ppermute | solution.py:96
  1183.2 31.9 %collective-permute-start.33 = (f32[128,2560]{1,0:T(8,128)S(1)}, f32[128,2560]{1,0:T(8,128)S(1)}, u32[]{:S(2)}, u32[]{:S(2)}) collective-permute-start(f32[128,2560]{1,0:T(8,128)S(1)} %collective-permute-done.32.rest_6_), channel_id=1, source_target_pairs={{0,1},{1,0},{2,3},{3,2},{4,5},{5,4},{6,7},{7,6}} | collective-permute-start | bytes 3932168 | tf_op jit(solution)/shard_map/ppermute | solution.py:96
  1196.1 65.9 %collective-permute-start.25 = (f32[1024,1024]{1,0:T(8,128)}, f32[1024,1024]{1,0:T(8,128)}, u32[]{:S(2)}, u32[]{:S(2)}) collective-permute-start(f32[1024,1024]{1,0:T(8,128)} %fusion.142.share_ref), channel_id=1, source_target_pairs={{0,1},{1,0},{2,3},{3,2},{4,5},{5,4},{6,7},{7,6}} | collective-permute-start | bytes 12582920 | tf_op jit(solution)/shard_map/ppermute | solution.py:232
  1197.3 36.9 %collective-permute-start.38 = (f32[128,3072]{1,0:T(8,128)S(1)}, f32[128,3072]{1,0:T(8,128)}, u32[]{:S(2)}, u32[]{:S(2)}) collective-permute-start(f32[128,3072]{1,0:T(8,128)S(1)} %copy-done.8), channel_id=1, source_target_pairs={{0,2},{2,0},{1,3},{3,1},{4,6},{6,4},{5,7},{7,5}} | collective-permute-start | bytes 4718600 | tf_op jit(solution)/shard_map/ppermute | solution.py:93
  1198.6 35.6 %collective-permute-start.21 = (f32[512,1024]{1,0:T(8,128)S(1)}, f32[512,1024]{1,0:T(8,128)S(1)}, u32[]{:S(2)}, u32[]{:S(2)}) collective-permute-start(f32[512,1024]{1,0:T(8,128)S(1)} %pad_maximum_fusion.13), channel_id=1, source_target_pairs={{0,1},{1,0},{2,3},{3,2},{4,5},{5,4},{6,7},{7,6}} | collective-permute-start | bytes 6291464 | tf_op jit(solution)/shard_map/ppermute | solution.py:227
  1200.0 63.6 %collective-permute-start.27 = (f32[1024,1024]{1,0:T(8,128)}, f32[1024,1024]{1,0:T(8,128)}, u32[]{:S(2)}, u32[]{:S(2)}) collective-permute-start(f32[1024,1024]{1,0:T(8,128)} %fusion.134.share_ref), channel_id=1, source_target_pairs={{0,1},{1,0},{2,3},{3,2},{4,5},{5,4},{6,7},{7,6}} | collective-permute-start | bytes 12582920 | tf_op jit(solution)/shard_map/ppermute | solution.py:232
  1215.1 65.9 %collective-permute-start.24 = (f32[1024,1024]{1,0:T(8,128)}, f32[1024,1024]{1,0:T(8,128)}, u32[]{:S(2)}, u32[]{:S(2)}) collective-permute-start(f32[1024,1024]{1,0:T(8,128)} %fusion.150.share_ref), channel_id=1, source_target_pairs={{0,1},{1,0},{2,3},{3,2},{4,5},{5,4},{6,7},{7,6}} | collective-permute-start | bytes 12582920 | tf_op jit(solution)/shard_map/ppermute | solution.py:232
  1234.2 9.4 collective-permute-start.37
  1235.5 25.3 %collective-permute-start.39 = (f32[128,3072]{1,0:T(8,128)}, f32[128,3072]{1,0:T(8,128)}, u32[]{:S(2)}, u32[]{:S(2)}) collective-permute-start(f32[128,3072]{1,0:T(8,128)} %collective-permute-done.38.rest_2_), channel_id=1, source_target_pairs={{0,1},{1,0},{2,3},{3,2},{4,5},{5,4},{6,7},{7,6}} | collective-permute-start | bytes 4718600 | tf_op jit(solution)/shard_map/ppermute | solution.py:96
  1243.6 37.3 %collective-permute-start.35 = (f32[128,3072]{1,0:T(8,128)S(1)}, f32[128,3072]{1,0:T(8,128)S(1)}, u32[]{:S(2)}, u32[]{:S(2)}) collective-permute-start(f32[128,3072]{1,0:T(8,128)S(1)} %pad_maximum_fusion.15.rest_0_), channel_id=1, source_target_pairs={{0,2},{2,0},{1,3},{3,1},{4,6},{6,4},{5,7},{7,5}} | collective-permute-start | bytes 4718600 | tf_op jit(solution)/shard_map/ppermute | solution.py:93
  1260.8 162.4 %collective-permute-start.26 = (f32[1024,1024]{1,0:T(8,128)}, f32[1024,1024]{1,0:T(8,128)}, u32[]{:S(2)}, u32[]{:S(2)}) collective-permute-start(f32[1024,1024]{1,0:T(8,128)} %fusion.158.share_ref), channel_id=1, source_target_pairs={{0,1},{1,0},{2,3},{3,2},{4,5},{5,4},{6,7},{7,6}} | collective-permute-start | bytes 12582920 | tf_op jit(solution)/shard_map/ppermute | solution.py:232
  1262.0 46.2 %collective-permute-start.41 = (f32[128,2560]{1,0:T(8,128)}, f32[128,2560]{1,0:T(8,128)}, u32[]{:S(2)}, u32[]{:S(2)}) collective-permute-start(f32[128,2560]{1,0:T(8,128)} %slice.149.rest_0_), channel_id=1, source_target_pairs={{0,2},{2,0},{1,3},{3,1},{4,6},{6,4},{5,7},{7,5}} | collective-permute-start | bytes 3932168 | tf_op jit(solution)/shard_map/ppermute | solution.py:93
  1263.7 49.3 %collective-permute-start.34 = (f32[128,3072]{1,0:T(8,128)S(1)}, f32[128,3072]{1,0:T(8,128)S(1)}, u32[]{:S(2)}, u32[]{:S(2)}) collective-permute-start(f32[128,3072]{1,0:T(8,128)S(1)} %pad_maximum_fusion.15.rest_0_), channel_id=1, source_target_pairs={{0,1},{1,0},{2,3},{3,2},{4,5},{5,4},{6,7},{7,6}} | collective-permute-start | bytes 4718600 | tf_op jit(solution)/shard_map/ppermute | solution.py:96
  1280.9 72.0 %copy-start.5 = (f32[128,3072]{1,0:T(8,128)}, f32[128,3072]{1,0:T(8,128)S(1)}, u32[]{:S(2)}) copy-start(f32[128,3072]{1,0:T(8,128)S(1)} %collective-permute-done.35.rest_2_) | copy-start | bytes 4718596
  1280.9 59.6 %collective-permute-start.36 = (f32[128,3072]{1,0:T(8,128)S(1)}, f32[128,3072]{1,0:T(8,128)S(1)}, u32[]{:S(2)}, u32[]{:S(2)}) collective-permute-start(f32[128,3072]{1,0:T(8,128)S(1)} %collective-permute-done.35.rest_2_), channel_id=1, source_target_pairs={{0,1},{1,0},{2,3},{3,2},{4,5},{5,4},{6,7},{7,6}} | collective-permute-start | bytes 4718600 | tf_op jit(solution)/shard_map/ppermute | solution.py:96
  1280.9 32.0 %collective-permute-start.43 = (f32[128,2560]{1,0:T(8,128)}, f32[128,2560]{1,0:T(8,128)}, u32[]{:S(2)}, u32[]{:S(2)}) collective-permute-start(f32[128,2560]{1,0:T(8,128)} %slice.149.rest_0_), channel_id=1, source_target_pairs={{0,4},{4,0},{1,5},{5,1},{2,6},{6,2},{3,7},{7,3}} | collective-permute-start | bytes 3932168 | tf_op jit(solution)/shard_map/ppermute | solution.py:95
  1308.2 32.4 %collective-permute-start.45 = (f32[128,2560]{1,0:T(8,128)}, f32[128,2560]{1,0:T(8,128)}, u32[]{:S(2)}, u32[]{:S(2)}) collective-permute-start(f32[128,2560]{1,0:T(8,128)} %collective-permute-done.41.rest_2_), channel_id=1, source_target_pairs={{0,4},{4,0},{1,5},{5,1},{2,6},{6,2},{3,7},{7,3}} | collective-permute-start | bytes 3932168 | tf_op jit(solution)/shard_map/ppermute | solution.py:95
  1312.9 121.1 %collective-permute-start.40 = (f32[128,2560]{1,0:T(8,128)}, f32[128,2560]{1,0:T(8,128)}, u32[]{:S(2)}, u32[]{:S(2)}) collective-permute-start(f32[128,2560]{1,0:T(8,128)} %slice.149.rest_0_), channel_id=1, source_target_pairs={{0,1},{1,0},{2,3},{3,2},{4,5},{5,4},{6,7},{7,6}} | collective-permute-start | bytes 3932168 | tf_op jit(solution)/shard_map/ppermute | solution.py:96
  1312.9 121.0 %collective-permute-start.42 = (f32[128,2560]{1,0:T(8,128)}, f32[128,2560]{1,0:T(8,128)S(1)}, u32[]{:S(2)}, u32[]{:S(2)}) collective-permute-start(f32[128,2560]{1,0:T(8,128)} %collective-permute-done.41.rest_2_), channel_id=1, source_target_pairs={{0,1},{1,0},{2,3},{3,2},{4,5},{5,4},{6,7},{7,6}} | collective-permute-start | bytes 3932168 | tf_op jit(solution)/shard_map/ppermute | solution.py:96
  1340.5 93.5 %collective-permute-start.44 = (f32[128,2560]{1,0:T(8,128)}, f32[128,2560]{1,0:T(8,128)}, u32[]{:S(2)}, u32[]{:S(2)}) collective-permute-start(f32[128,2560]{1,0:T(8,128)} %collective-permute-done.43.rest_4_), channel_id=1, source_target_pairs={{0,1},{1,0},{2,3},{3,2},{4,5},{5,4},{6,7},{7,6}} | collective-permute-start | bytes 3932168 | tf_op jit(solution)/shard_map/ppermute | solution.py:96
  1341.7 92.3 %collective-permute-start.46 = (f32[128,2560]{1,0:T(8,128)}, f32[128,2560]{1,0:T(8,128)}, u32[]{:S(2)}, u32[]{:S(2)}) collective-permute-start(f32[128,2560]{1,0:T(8,128)} %collective-permute-done.45.rest_6_), channel_id=1, source_target_pairs={{0,1},{1,0},{2,3},{3,2},{4,5},{5,4},{6,7},{7,6}} | collective-permute-start | bytes 3932168 | tf_op jit(solution)/shard_map/ppermute | solution.py:96
  (39 other events, 409.1 us)
Sparse Core Ops, SparseCore 0:
  81.7 81.6 reduce-scatter.8
  307.8 65.6 reduce-scatter.10
  432.4 106.9 reduce-scatter.12
  625.5 68.2 reduce-scatter.14
  696.2 53.3 reduce-scatter.20
  757.8 77.0 reduce-scatter.18
  857.4 87.5 reduce-scatter.16
  974.9 73.1 reduce-scatter.22

commit v3 on v2

--- a/solution.py
+++ b/solution.py
@@ -256,8 +256,8 @@
         h_three_own = activate(z_three[:, OWN])
         dw_four_part = matmul_tn(h_three_own, dy_tokens)
         dw_four = sum_scatter(dw_four_part)
-        g_three = back_gate(matmul_nt(after(dy_tokens, dw_four_part, edge_all[2]), weight_four).astype(jnp.bfloat16), z_three)
-        g_three = after(g_three, early_sum, edge_all[4], edge_all[6])
+        g_three = back_gate(matmul_nt(after(dy_tokens, dw_four_part), weight_four).astype(jnp.bfloat16), z_three)
+        g_three = after(g_three, early_sum, edge_all[2], edge_all[4])
         h_two_all = spread(early_sum[:, block_cols:], True)
         g_three_own = g_three[:, OWN]
         dw_three_part = matmul_tn(g_three_own, h_two)
@@ -269,7 +269,7 @@
         dw_two_part = matmul_tn(h_one_own, g_two)
         dw_two = sum_scatter(dw_two_part)
         done_three = wide_product(after(dw_three, dw_two_part), a_inv_col[1])
-        g_one_own = back_gate(matmul_nt(after(g_two, done_three[0], h_two_all[2]), w_row[0]).astype(jnp.bfloat16), z_one[:, OWN])
+        g_one_own = back_gate(matmul_nt(after(g_two, done_three[0], h_two_all[2], edge_all[6]), w_row[0]).astype(jnp.bfloat16), z_one[:, OWN])
         dw_one_part = matmul_tn(g_one_own, x_tokens)
         dw_one = sum_scatter(dw_one_part)
         g_two_late = after(g_two, dw_one_part, middle_sum, done_four[1])
@@ -285,23 +285,23 @@
         a_new_col = blend_layer(a_old_col, edge_all, 0, 0, new_scale, spot, None)
         s_new_row = blend_layer(s_old_row, edge_all, 5, 1, new_scale, spot, None)
         col_three = block_product(done_three, s_inv_col[1], True, after(place, a_new_col, s_new_row))
-        done_one = wide_product(after(dw_one, col_three[0], a_new_col, s_new_row), a_inv_col[0])
-        spot = after(place, done_one[0])
+        spot = after(place, col_three[0])
+        u_row = join_layer(*row_four, 1, False, spot, None)
+        u_col = join_layer(*col_three, 1, True, spot, None)
         a_new_col = blend_layer(a_old_col, h_two_all, 0, 1, new_scale, spot, a_new_col)
         a_new_row = blend_layer(a_old_row, mid_all, 0, 1, new_scale, spot, None)
         s_new_col = blend_layer(s_old_col, mid_all, 3, 1, new_scale, spot, None)
-        u_row = join_layer(*row_four, 1, False, spot, None)
-        u_col = join_layer(*col_three, 1, True, spot, None)
         outer_all = spread(jnp.concatenate([early_sum[:, :block_cols], late_sum[:, full_cols:]], 1), False)
         g_two_all = spread(late_sum[:, :full_cols], True)
-        row_two = block_product(done_two, a_inv_row[0], False, after(place, a_new_col, u_row, u_col, late_sum))
-        col_one = block_product(done_one, s_inv_col[0], True, row_two[0])
-        spot = after(place, col_one[0])
-        u_row = join_layer(*row_two, 0, False, spot, u_row)
+        done_one = wide_product(after(dw_one, a_new_col, a_new_row, s_new_col, u_row, u_col), a_inv_col[0])
+        row_two = block_product(done_two, a_inv_row[0], False, done_one[0])
+        spot = after(place, row_two[0])
         a_new_row = blend_layer(a_old_row, outer_all, 0, 0, new_scale, spot, a_new_row)
         s_new_col = blend_layer(s_old_col, outer_all, 3, 0, new_scale, spot, s_new_col)
-        u_col = join_layer(*col_one, 0, True, after(spot, u_row), u_col)
-        s_new_row = blend_layer(s_old_row, g_two_all, 0, 0, new_scale, after(spot, u_col), s_new_row)
+        u_row = join_layer(*row_two, 0, False, after(spot, a_new_row, s_new_col), u_row)
+        s_new_row = blend_layer(s_old_row, g_two_all, 0, 0, new_scale, after(spot, u_row), s_new_row)
+        col_one = block_product(done_one, s_inv_col[0], True, s_new_row)
+        u_col = join_layer(*col_one, 0, True, place, u_col)
         return (u_col, u_row, a_new_col, s_new_col, a_new_row, s_new_row)
 
     batch_split = P('data', None)

time: 1480 us -> 1520 us (1.027)
  waiting for transfers between devices: 430 us -> 454 us
    ppermute x4, waiting for transfers between devices: 90.8 us -> 114 us  [wide_product(): return (done, lax.ppermute(done, 'data', CHIP_SWAP))]
  transfers between devices with their start and end apart: 55 -> 55, of which waited for: 14 -> 13; matrix products, arithmetic and copies ran while one was open for 44% -> 43% of each run, Pallas kernels for 9% -> 8%
where the time goes in v3:
time: 1520 us; the launch traced here: 1510 us
  matrix products  657 us (43%)
  waiting for transfers between devices  454 us (30%)
  Pallas kernels  162 us (11%)
  local copies, waits for them, and re-layouts  125 us (8%)
  other arithmetic  61.6 us (4%)
  starting transfers between devices  33.8 us (2%)
  between operations  15.5 us (1%)
    dot_general x20, matrix products, matmul_tn(): lax.dot_general(left_mat, right_mat, TN_DIMS, preferred_element_type=jnp....  218 us
    ppermute x5, waiting for transfers between devices, spread(): found = [piece, lax.ppermute(piece, 'data', CHIP_SWAP)]  173 us
    dot_general x3, matrix products, matmul_nt(): lax.dot_general(left_mat, right_mat, NT_DIMS, preferred_element_type=jnp....  157 us
    dot_general x3, matrix products, matmul(): return jnp.dot(left_mat, right_mat, preferred_element_type=jnp.float32)  147 us
    pallas_call x8, Pallas kernels, blend_layer(): pl.pallas_call(functools.partial(blend_body, new_scale, blocks, groups),...  118 us
    ppermute x4, waiting for transfers between devices, wide_product(): return (done, lax.ppermute(done, 'data', CHIP_SWAP))  114 us
    ppermute x4, waiting for transfers between devices, weight_piece(): lax.ppermute(lax.dynamic_slice(stack, starts, sizes)[0], 'model', MODEL_S...  92.8 us
    dot_general x4, matrix products, exact_dot(): jnp.dot(left_mat, right_mat, precision=EXACT, preferred_element_type=jnp....  74.5 us
  transfers between devices with their start and end apart: 55, of which 13 were waited for; matrix products, arithmetic and copies ran while one was open for 43% of the time, Pallas kernels for 8%

profile of v3, /device:TPU:0, one launch (start us, length us, event | category | flops | bytes accessed | tf_op | source)
XLA Modules:
  0.0 1508.0 jit_solution(3801838973294964059)
XLA Ops:
  7.2 22.6 %constant_dynamic-slice_fusion.26 = (bf16[4096,512]{1,0:T(8,128)(2,1)}, bf16[4096,512]{1,0:T(8,128)(2,1)}, bf16[4096,512]{1,0:T(8,128)(2,1)}, bf16[4096,512]{1,0...) fusion(bf16[4096,2048]{1,0:T(8,128)(2,1)} %param.37, ...), kind=kLoop, calls=%fused_computation.279 | loop fusion | bytes 67108880 | tf_op jit(solution)/shard_map/dynamic_slice | solution.py:71
  29.8 10.5 fusion.88
  40.3 11.3 fusion.66
  51.7 10.6 fusion.84
  62.2 10.8 fusion.60
  73.1 7.5 pad_maximum_fusion
  88.1 45.6 %collective-permute-done = bf16[2048,512]{1,0:T(8,128)(2,1)S(1)} collective-permute-done((bf16[2048,512]{1,0:T(8,128)(2,1)S(1)}, bf16[2048,512]{1,0:T(8,128)(2,1)S(1)}, u32[]{:S(2)}, u32[]{:S(2)}) %collective-permute-start) | collective-permute-done | bytes 2097184 | tf_op jit(solution)/shard_map/ppermute | solution.py:208
  133.7 5.1 dynamic-slice_bitcast_fusion
  146.6 53.2 %fusion.17 = (bf16[4096,2048]{1,0:T(8,128)(2,1)}, bf16[4096,2048]{1,0:T(8,128)(2,1)}) fusion(bf16[4096,2048]{1,0:T(8,128)(2,1)} %param.36, bf16[2048,512]{1,0:T(8,128)(2,1)} %get-tuple-element.103, bf16[2048,1024]{1,0:T(8,128)(2,1)} %get-tuple-element.77, bf16[2048,512]{1,0:T(8,128)(2,1)} %get-tuple-element.102), kind=kOutput, calls=%fused_computation.35 | convolution fusion | flops 34468790272 | bytes 58720256 | tf_op jit(solution)/shard_map/dot_general | solution.py:50
  199.8 7.5 slice_bitcast_fusion
  213.3 5.8 fusion.117
  221.7 52.6 %fusion.25 = (bf16[4096,2048]{1,0:T(8,128)(2,1)}, bf16[4096,2048]{1,0:T(8,128)(2,1)}) fusion(bf16[4096,2048]{1,0:T(8,128)(2,1)} %get-tuple-element.30, bf16[512,2048]{1,0:T(8,128)(2,1)} %get-tuple-element.101, bf16[1024,2048]{1,0:T(8,128)(2,1)} %get-tuple-element.73, bf16[512,2048]{1,0:T(8,128)(2,1)} %get-tuple-element.100), kind=kOutput, calls=%fused_computation.43 | convolution fusion | flops 34468790272 | bytes 58720256 | tf_op jit(solution)/shard_map/dot_general | solution.py:50
  274.3 8.7 constant_dynamic-slice_fusion.22
  283.0 5.8 fusion.102
  288.9 12.0 fusion.72
  300.9 5.9 pad_maximum_fusion.1
  308.7 47.2 %collective-permute-done.4 = bf16[2048,512]{1,0:T(8,128)(2,1)S(1)} collective-permute-done((bf16[2048,512]{1,0:T(8,128)(2,1)S(1)}, bf16[2048,512]{1,0:T(8,128)(2,1)S(1)}, u32[]{:S(2)}, u32[]{:S(2)}) %collective-permute-start.4) | collective-permute-done | bytes 2097184 | tf_op jit(solution)/shard_map/ppermute | solution.py:208
  360.4 41.1 %convolution_convert_fusion = bf16[4096,2048]{1,0:T(8,128)(2,1)} fusion(bf16[4096,2048]{1,0:T(8,128)(2,1)} %get-tuple-element.32, bf16[2048,512]{1,0:T(8,128)(2,1)S(1)} %get-tuple-element.99, bf16[2048,1024]{1,0:T(8,128)(2,1)S(1)} %copy-done.18, bf16[2048,512]{1,0:T(8,128)(2,1)S(1)} %get-tuple-element.98), kind=kOutput, calls=%fused_computation.87 | convolution fusion | flops 34393292800 | bytes 41943040 | tf_op jit(solution)/shard_map/dot_general | solution.py:50
  401.5 29.9 %fusion.198 = f32[1024,2048]{1,0:T(8,128)} fusion(bf16[4096,2048]{1,0:T(8,128)(2,1)} %param.37, bf16[4096,2048]{1,0:T(8,128)(2,1)} %convolution_convert_fusion), kind=kOutput, calls=%fused_computation.307 | convolution fusion | flops 17217617920 | bytes 33554432 | tf_op jit(solution)/shard_map/dot_general | solution.py:54
  437.5 5.0 broadcast_select_fusion.1
  442.5 63.8 %fusion.13 = bf16[4096,2048]{1,0:T(8,128)(2,1)} fusion(bf16[4096,2048]{1,0:T(8,128)(2,1)} %convolution_convert_fusion, bf16[4096,2048]{1,0:T(8,128)(2,1)} %param.37, bf16[512,2048]{1,0:T(8,128)(2,1)} %get-tuple-element.97, bf16[1024,2048]{1,0:T(8,128)(2,1)} %get-tuple-element.72, bf16[512,2048]{1,0:T(8,128)(2,1)} %get-tuple-element.96), kind=kOutput, calls=%fused_computation.31 | convolution fusion | flops 34544287744 | bytes 58720256 | tf_op jit(solution)/shard_map/dot_general | solution.py:58
  506.3 27.7 %collective-permute-done.8.rest_2_ = f32[128,5120]{1,0:T(8,128)} collective-permute-done((f32[128,5120]{1,0:T(8,128)S(1)}, f32[128,5120]{1,0:T(8,128)}, u32[]{:S(2)}, u32[]{:S(2)}) %collective-permute-start.8) | collective-permute-done | bytes 2621472 | tf_op jit(solution)/shard_map/ppermute | solution.py:93
  534.1 24.7 %fusion.121 = f32[1024,2048]{1,0:T(8,128)} fusion(bf16[4096,2048]{1,0:T(8,128)(2,1)} %fusion.13, bf16[4096,2048]{1,0:T(8,128)(2,1)} %get-tuple-element.123), kind=kOutput, calls=%fused_computation.155 | convolution fusion | flops 17255366656 | bytes 33554432 | tf_op jit(solution)/shard_map/dot_general | solution.py:54
  558.8 7.7 fusion.41
  577.3 4.5 fusion.119
  584.8 19.0 %fusion.54 = f32[256,2048]{1,0:T(8,128)} fusion(f32[2,2048,2048]{2,1,0:T(8,128)} %param.47, f32[256,2048]{1,0:T(8,128)} %reduce-scatter.13.cloned.1.call-done), kind=kOutput, calls=%fused_computation.81 | convolution fusion | flops 12885426176 | bytes 20971520 | tf_op jit(solution)/shard_map/dot_general | solution.py:62
  603.8 62.3 %fusion.8 = bf16[4096,2048]{1,0:T(8,128)(2,1)} fusion(bf16[4096,2048]{1,0:T(8,128)(2,1)} %get-tuple-element.123, bf16[4096,2048]{1,0:T(8,128)(2,1)} %fusion.13, bf16[2048,512]{1,0:T(8,128)(2,1)} %copy-done.32, bf16[2048,1024]{1,0:T(8,128)(2,1)} %get-tuple-element.76, bf16[2048,512]{1,0:T(8,128)(2,1)S(1)} %copy-done.31), kind=kOutput, calls=%fused_computation.26 | convolution fusion | flops 34544287744 | bytes 58720256 | tf_op jit(solution)/shard_map/dot_general | solution.py:58
  666.1 24.1 %fusion.115 = f32[1024,2048]{1,0:T(8,128)} fusion(bf16[4096,2048]{1,0:T(8,128)(2,1)} %fusion.8, bf16[4096,2048]{1,0:T(8,128)(2,1)} %get-tuple-element.30), kind=kOutput, calls=%fused_computation.149 | convolution fusion | flops 17179869184 | bytes 33554432 | tf_op jit(solution)/shard_map/dot_general | solution.py:54
  694.2 19.4 %fusion.52 = f32[256,2048]{1,0:T(8,128)} fusion(f32[2,2048,2048]{2,1,0:T(8,128)} %param.44, f32[256,2048]{1,0:T(8,128)} %reduce-scatter.15.cloned.1.call-done), kind=kOutput, calls=%fused_computation.79 | convolution fusion | flops 12885426176 | bytes 20971520 | tf_op jit(solution)/shard_map/dot_general | solution.py:62
  713.6 34.2 %collective-permute-done.11.rest_6_ = f32[128,5120]{1,0:T(8,128)} collective-permute-done((f32[128,5120]{1,0:T(8,128)}, f32[128,5120]{1,0:T(8,128)}, u32[]{:S(2)}, u32[]{:S(2)}) %collective-permute-start.11) | collective-permute-done | bytes 2621472 | tf_op jit(solution)/shard_map/ppermute | solution.py:95
  747.8 30.9 %fusion.38 = bf16[4096,1024]{1,0:T(8,128)(2,1)S(1)} fusion(bf16[4096,2048]{1,0:T(8,128)(2,1)} %get-tuple-element.121, bf16[4096,2048]{1,0:T(8,128)(2,1)} %fusion.8, bf16[2,1024,2048]{2,1,0:T(8,128)(2,1)} %param.39), kind=kOutput, calls=%fused_computation.65 | convolution fusion | flops 17259560960 | bytes 37748736 | tf_op jit(solution)/shard_map/dot_general | solution.py:58
  782.2 21.8 %fusion.203 = f32[1024,2048]{1,0:T(8,128)} fusion(bf16[4096,1024]{1,0:T(8,128)(2,1)S(1)} %fusion.38, bf16[4096,2048]{1,0:T(8,128)(2,1)} %param.36), kind=kOutput, calls=%fused_computation.310 | convolution fusion | flops 17179869184 | bytes 33554432 | tf_op jit(solution)/shard_map/dot_general | solution.py:54
  808.3 74.7 %collective-permute-done.20 = f32[256,2048]{1,0:T(8,128)} collective-permute-done((f32[256,2048]{1,0:T(8,128)S(1)}, f32[256,2048]{1,0:T(8,128)}, u32[]{:S(2)}, u32[]{:S(2)}) %collective-permute-start.20) | collective-permute-done | bytes 2097184 | tf_op jit(solution)/shard_map/ppermute | solution.py:222
  882.9 5.8 fusion.123
  888.8 8.7 constant_dynamic-slice_fusion.10
  897.5 5.8 fusion.111
  903.3 10.5 fusion.125
  913.8 12.0 fusion.78
  925.8 6.2 pad_maximum_fusion.3
  943.1 7.4 fusion.201
  951.0 7.5 fusion.202
  959.7 39.3 %collective-permute-done.12 = f32[256,2048]{1,0:T(8,128)} collective-permute-done((f32[256,2048]{1,0:T(8,128)}, f32[256,2048]{1,0:T(8,128)}, u32[]{:S(2)}, u32[]{:S(2)}) %collective-permute-start.12) | collective-permute-done | bytes 2097184 | tf_op jit(solution)/shard_map/ppermute | solution.py:222
  1012.2 17.5 %fusion.50 = f32[256,2048]{1,0:T(8,128)S(1)} fusion(f32[2,2048,2048]{2,1,0:T(8,128)} %param.47, f32[256,2048]{1,0:T(8,128)} %reduce-scatter.19.cloned.1.call-done), kind=kOutput, calls=%fused_computation.77 | convolution fusion | flops 12885426176 | bytes 20971520 | tf_op jit(solution)/shard_map/dot_general | solution.py:62
  1032.4 14.9 fusion.142.share_ref
  1050.6 15.2 %fusion.134.share_ref = f32[1024,1024]{1,0:T(8,128)} fusion(f32[1024,1024]{1,0:T(8,128)S(1)} %pad_maximum_fusion.5, f32[256,1024]{1,0:T(8,128)S(1)} %copy-done.42, f32[256,1024]{1,0:T(8,128)S(1)} %copy-done.43, f32[256,1024]{1,0:T(8,128)S(1)} %copy-done.44, f32[256,1024]{1,0:T(8,128)S(1)} %copy-done.41), kind=kOutput, calls=%fused_computation.170 | convolution fusion | flops 12888047616 | bytes 12582912 | tf_op jit(solution)/shard_map/dot_general | solution.py:66
  1067.9 44.6 %collective-permute-done.27.rest_2_ = f32[128,3072]{1,0:T(8,128)S(1)} collective-permute-done((f32[128,3072]{1,0:T(8,128)S(1)}, f32[128,3072]{1,0:T(8,128)S(1)}, u32[]{:S(2)}, u32[]{:S(2)}) %collective-permute-start.27) | collective-permute-done | bytes 1572896 | tf_op jit(solution)/shard_map/ppermute | solution.py:93
  1123.3 23.3 %blend_layer.8.rest_8_ = f32[2,2048,2048]{2,1,0:T(8,128)} custom-call(s32[16]{0:T(128)} %constant.78.clone.half_tab, s32[16]{0:T(128)} %constant.79.clone.piece_tab, s32[16]{0:T(128)} %constant.80.clone.flip_tab, s32[2]{0:T(128)} %pad_add_fusion.place, f32[2,2048,2048]{2,1,0:T(8,128)} %old_ref.9, f32[128,5120]{1,0:T(8,128)} %reduce-scatter.9.cloned.1.call-done.rest_0_, ...), custom_call_target="tpu_custom_call" | custom-call | flops 12582912 | bytes 50331648 | tf_op jit(solution)/shard_map/blend_layer/pallas_call | solution.py:145
  1147.0 6.2 blend_layer.10.rest_4_
  1153.3 6.2 blend_layer.11.rest_4_
  1160.5 23.5 %blend_layer.9 = f32[2,2048,2048]{2,1,0:T(8,128)} custom-call(s32[16]{0:T(128)} %constant.78.clone.half_tab, s32[16]{0:T(128)} %constant.79.clone.piece_tab, s32[16]{0:T(128)} %constant.80.clone.flip_tab, s32[2]{0:T(128)} %pad_add_fusion.place, f32[2,2048,2048]{2,1,0:T(8,128)} %old_ref.9, f32[128,2560]{1,0:T(8,128)} %copy-done.14, ...), custom_call_target="tpu_custom_call", output_to_operand_aliasing={{}: (13, {})} | custom-call | flops 12582912 | bytes 50331648 | tf_op jit(solution)/shard_map/blend_layer/pallas_call | solution.py:145
  1184.0 10.9 join_layer.4.rest_0_
  1199.1 10.8 join_layer.5.rest_0_
  1209.9 18.7 %fusion.48 = f32[256,2048]{1,0:T(8,128)} fusion(f32[2,2048,2048]{2,1,0:T(8,128)} %param.44, f32[256,2048]{1,0:T(8,128)} %reduce-scatter.17.cloned.1.call-done), kind=kOutput, calls=%fused_computation.75 | convolution fusion | flops 12885426176 | bytes 20971520 | tf_op jit(solution)/shard_map/dot_general | solution.py:62
  1228.7 15.2 %fusion.150.share_ref = f32[1024,1024]{1,0:T(8,128)} fusion(f32[1024,1024]{1,0:T(8,128)S(1)} %copy-done.17, f32[256,1024]{1,0:T(8,128)S(1)} %copy-done.47, f32[256,1024]{1,0:T(8,128)S(1)} %copy-done.46, f32[256,1024]{1,0:T(8,128)S(1)} %copy-done.45, f32[256,1024]{1,0:T(8,128)S(1)} %copy-done.48), kind=kOutput, calls=%fused_computation.188 | convolution fusion | flops 12888047616 | bytes 12582912 | tf_op jit(solution)/shard_map/dot_general | solution.py:66
  1253.6 100.5 %collective-permute-done.40.rest_2_ = f32[128,2560]{1,0:T(8,128)} collective-permute-done((f32[128,2560]{1,0:T(8,128)}, f32[128,2560]{1,0:T(8,128)}, u32[]{:S(2)}, u32[]{:S(2)}) %collective-permute-start.40) | collective-permute-done | bytes 1310752 | tf_op jit(solution)/shard_map/ppermute | solution.py:93
  1363.8 25.1 %collective-permute-done.44.rest_6_ = f32[128,2560]{1,0:T(8,128)} collective-permute-done((f32[128,2560]{1,0:T(8,128)}, f32[128,2560]{1,0:T(8,128)}, u32[]{:S(2)}, u32[]{:S(2)}) %collective-permute-start.44) | collective-permute-done | bytes 1310752 | tf_op jit(solution)/shard_map/ppermute | solution.py:95
  1390.6 23.3 %blend_layer.14.rest_8_ = f32[2,2048,2048]{2,1,0:T(8,128)} custom-call(s32[16]{0:T(128)} %constant.78.clone.half_tab, s32[16]{0:T(128)} %constant.79.clone.piece_tab, s32[16]{0:T(128)} %constant.80.clone.flip_tab, s32[2]{0:T(128)} %pad_add_fusion.place, f32[2,2048,2048]{2,1,0:T(8,128)} %old_ref.15, f32[128,5120]{1,0:T(8,128)} %reduce-scatter.9.cloned.1.call-done.rest_0_, ...), custom_call_target="tpu_custom_call" | custom-call | flops 12582912 | bytes 50331648 | tf_op jit(solution)/shard_map/blend_layer/pallas_call | solution.py:145
  1413.9 6.2 blend_layer.12
  1420.1 6.2 blend_layer.13
  1426.3 10.9 join_layer.6
  1441.4 23.4 %blend_layer.15 = f32[2,2048,2048]{2,1,0:T(8,128)} custom-call(s32[16]{0:T(128)} %constant.78.clone.half_tab, s32[16]{0:T(128)} %constant.79.clone.piece_tab, s32[16]{0:T(128)} %constant.80.clone.flip_tab, s32[2]{0:T(128)} %pad_add_fusion.place, f32[2,2048,2048]{2,1,0:T(8,128)} %old_ref.15, ...), custom_call_target="tpu_custom_call", output_to_operand_aliasing={{}: (13, {})} | custom-call | flops 12582912 | bytes 50331648 | tf_op jit(solution)/shard_map/blend_layer/pallas_call | solution.py:145
  1464.8 15.7 %fusion.158.share_ref = f32[1024,1024]{1,0:T(8,128)S(1)} fusion(f32[1024,1024]{1,0:T(8,128)} %pad_maximum_fusion.7, f32[256,1024]{1,0:T(8,128)S(1)} %copy-done.39, f32[256,1024]{1,0:T(8,128)S(1)} %copy-done.40, f32[256,1024]{1,0:T(8,128)} %get-tuple-element.83, f32[256,1024]{1,0:T(8,128)S(1)} %copy-done.38), kind=kOutput, calls=%fused_computation.197 | convolution fusion | flops 12888047616 | bytes 12582912 | tf_op jit(solution)/shard_map/dot_general | solution.py:66
  1482.6 7.3 collective-permute-done.46.other_ref
  1489.9 10.8 join_layer.7
  (269 shorter events, 139.3 us)
Async XLA Ops:
  7.2 214.5 %reduce-scatter.9.cloned.1.call-start = ((), (), s32[]{:S(2)}) async-start(), calls=%async_computation.8 | async-start | bytes 13107200 | tf_op jit(solution)/shard_map/reduce_scatter | solution.py:89
  80.6 453.4 %reduce-scatter.11.cloned.1.call-start = ((), (), s32[]{:S(2)}) async-start(), calls=%async_computation.9 | async-start | bytes 10485760 | tf_op jit(solution)/shard_map/reduce_scatter | solution.py:89
  80.7 59.8 %slice-start = ((s8[8388608]{0:T(1024)(128)(4,1)}), s8[4194304]{0:T(1024)(128)(4,1)S(1)}, s32[]{:S(2)}) async-start(s8[8388608]{0:T(1024)(128)(4,1)} %bitcast.87), calls=%async_computation.16 | async-start | bytes 8388608
  84.7 55.8 %slice-start.1 = ((s8[8388608]{0:T(1024)(128)(4,1)}), s8[4194304]{0:T(1024)(128)(4,1)S(1)}, s32[]{:S(2)}) async-start(s8[8388608]{0:T(1024)(128)(4,1)} %bitcast.87), calls=%async_computation.17 | async-start | bytes 8388608
  84.7 49.0 %collective-permute-start = (bf16[2048,512]{1,0:T(8,128)(2,1)S(1)}, bf16[2048,512]{1,0:T(8,128)(2,1)S(1)}, u32[]{:S(2)}, u32[]{:S(2)}) collective-permute-start(bf16[2048,512]{1,0:T(8,128)(2,1)S(1)} %get-tuple-element.79), channel_id=1, source_target_pairs={{0,4},{4,0},{1,5},{5,1},{2,6},{6,2},{3,7},{7,3}} | collective-permute-start | bytes 6291464 | tf_op jit(solution)/shard_map/ppermute | solution.py:208
  133.7 10.6 collective-permute-start.1
  138.8 61.0 %collective-permute-start.2 = (bf16[512,2048]{1,0:T(8,128)(2,1)}, bf16[512,2048]{1,0:T(8,128)(2,1)S(1)}, u32[]{:S(2)}, u32[]{:S(2)}) collective-permute-start(bf16[512,2048]{1,0:T(8,128)(2,1)} %get-tuple-element.75), channel_id=1, source_target_pairs={{0,4},{4,0},{1,5},{5,1},{2,6},{6,2},{3,7},{7,3}} | collective-permute-start | bytes 6291464 | tf_op jit(solution)/shard_map/ppermute | solution.py:208
  199.8 19.3 %collective-permute-start.3 = (bf16[512,2048]{1,0:T(8,128)(2,1)S(1)}, bf16[512,2048]{1,0:T(8,128)(2,1)S(1)}, u32[]{:S(2)}, u32[]{:S(2)}) collective-permute-start(bf16[512,2048]{1,0:T(8,128)(2,1)S(1)} %collective-permute-done.2), channel_id=1, source_target_pairs={{0,1},{1,0},{2,3},{3,2},{4,5},{5,4},{6,7},{7,6}} | collective-permute-start | bytes 6291464 | tf_op jit(solution)/shard_map/ppermute | solution.py:211
  306.8 278.0 %reduce-scatter.13.cloned.1.call-start = ((), (), s32[]{:S(2)}) async-start(), calls=%async_computation.10 | async-start | bytes 10485760 | tf_op jit(solution)/shard_map/reduce_scatter | solution.py:89
  306.8 53.5 %copy-start.18 = (bf16[2048,1024]{1,0:T(8,128)(2,1)S(1)}, bf16[2048,1024]{1,0:T(8,128)(2,1)}, u32[]{:S(2)}) copy-start(bf16[2048,1024]{1,0:T(8,128)(2,1)} %get-tuple-element.76) | copy-start | bytes 12582916
  308.4 47.5 %collective-permute-start.4 = (bf16[2048,512]{1,0:T(8,128)(2,1)S(1)}, bf16[2048,512]{1,0:T(8,128)(2,1)S(1)}, u32[]{:S(2)}, u32[]{:S(2)}) collective-permute-start(bf16[2048,512]{1,0:T(8,128)(2,1)S(1)} %copy-done.29), channel_id=1, source_target_pairs={{0,4},{4,0},{1,5},{5,1},{2,6},{6,2},{3,7},{7,3}} | collective-permute-start | bytes 6291464 | tf_op jit(solution)/shard_map/ppermute | solution.py:208
  355.9 4.2 collective-permute-start.5
  355.9 75.6 %collective-permute-start.6 = (bf16[512,2048]{1,0:T(8,128)(2,1)}, bf16[512,2048]{1,0:T(8,128)(2,1)}, u32[]{:S(2)}, u32[]{:S(2)}) collective-permute-start(bf16[512,2048]{1,0:T(8,128)(2,1)} %get-tuple-element.74), channel_id=1, source_target_pairs={{0,4},{4,0},{1,5},{5,1},{2,6},{6,2},{3,7},{7,3}} | collective-permute-start | bytes 6291464 | tf_op jit(solution)/shard_map/ppermute | solution.py:208
  431.4 262.8 %reduce-scatter.15.cloned.1.call-start = ((), (), s32[]{:S(2)}) async-start(), calls=%async_computation.11 | async-start | bytes 10485760 | tf_op jit(solution)/shard_map/reduce_scatter | solution.py:89
  431.5 6.1 collective-permute-start.7
  433.1 100.9 %collective-permute-start.8 = (f32[128,5120]{1,0:T(8,128)S(1)}, f32[128,5120]{1,0:T(8,128)}, u32[]{:S(2)}, u32[]{:S(2)}) collective-permute-start(f32[128,5120]{1,0:T(8,128)S(1)} %copy-done.3), channel_id=1, source_target_pairs={{0,2},{2,0},{1,3},{3,1},{4,6},{6,4},{5,7},{7,5}} | collective-permute-start | bytes 7864328 | tf_op jit(solution)/shard_map/ppermute | solution.py:93
  434.5 99.5 %collective-permute-start.9 = (f32[128,5120]{1,0:T(8,128)S(1)}, f32[128,5120]{1,0:T(8,128)}, u32[]{:S(2)}, u32[]{:S(2)}) collective-permute-start(f32[128,5120]{1,0:T(8,128)S(1)} %copy-done.3), channel_id=1, source_target_pairs={{0,4},{4,0},{1,5},{5,1},{2,6},{6,2},{3,7},{7,3}} | collective-permute-start | bytes 7864328 | tf_op jit(solution)/shard_map/ppermute | solution.py:95
  558.7 324.2 %reduce-scatter.21.cloned.1.call-start = ((), (), s32[]{:S(2)}) async-start(), calls=%async_computation.14 | async-start | bytes 7864320 | tf_op jit(solution)/shard_map/reduce_scatter | solution.py:89
  584.7 427.4 %reduce-scatter.19.cloned.1.call-start = ((), (), s32[]{:S(2)}) async-start(), calls=%async_computation.13 | async-start | bytes 10485760 | tf_op jit(solution)/shard_map/reduce_scatter | solution.py:89
  690.2 519.7 %reduce-scatter.17.cloned.1.call-start = ((), (), s32[]{:S(2)}) async-start(), calls=%async_computation.12 | async-start | bytes 10485760 | tf_op jit(solution)/shard_map/reduce_scatter | solution.py:89
  690.3 57.6 %collective-permute-start.11 = (f32[128,5120]{1,0:T(8,128)}, f32[128,5120]{1,0:T(8,128)}, u32[]{:S(2)}, u32[]{:S(2)}) collective-permute-start(f32[128,5120]{1,0:T(8,128)} %collective-permute-done.8.rest_2_), channel_id=1, source_target_pairs={{0,4},{4,0},{1,5},{5,1},{2,6},{6,2},{3,7},{7,3}} | collective-permute-start | bytes 7864328 | tf_op jit(solution)/shard_map/ppermute | solution.py:95
  691.9 55.9 %collective-permute-start.10 = (f32[128,2560]{1,0:T(8,128)S(1)}, f32[128,2560]{1,0:T(8,128)S(1)}, u32[]{:S(2)}, u32[]{:S(2)}) collective-permute-start(f32[128,2560]{1,0:T(8,128)S(1)} %slice.143.rest_0_), channel_id=1, source_target_pairs={{0,2},{2,0},{1,3},{3,1},{4,6},{6,4},{5,7},{7,5}} | collective-permute-start | bytes 3932168 | tf_op jit(solution)/shard_map/ppermute | solution.py:93
  804.0 442.1 %reduce-scatter.23.cloned.1.call-start = ((), (), s32[]{:S(2)}) async-start(), calls=%async_computation.15 | async-start | bytes 10485760 | tf_op jit(solution)/shard_map/reduce_scatter | solution.py:89
  805.5 77.4 %collective-permute-start.20 = (f32[256,2048]{1,0:T(8,128)S(1)}, f32[256,2048]{1,0:T(8,128)}, u32[]{:S(2)}, u32[]{:S(2)}) collective-permute-start(f32[256,2048]{1,0:T(8,128)S(1)} %copy-done.6), channel_id=1, source_target_pairs={{0,2},{2,0},{1,3},{3,1},{4,6},{6,4},{5,7},{7,5}} | collective-permute-start | bytes 6291464 | tf_op jit(solution)/shard_map/ppermute | solution.py:222
  932.0 67.0 %collective-permute-start.12 = (f32[256,2048]{1,0:T(8,128)}, f32[256,2048]{1,0:T(8,128)}, u32[]{:S(2)}, u32[]{:S(2)}) collective-permute-start(f32[256,2048]{1,0:T(8,128)} %fusion.52), channel_id=1, source_target_pairs={{0,2},{2,0},{1,3},{3,1},{4,6},{6,4},{5,7},{7,5}} | collective-permute-start | bytes 6291464 | tf_op jit(solution)/shard_map/ppermute | solution.py:222
  942.6 60.6 %collective-permute-start.21 = (f32[512,1024]{1,0:T(8,128)}, f32[512,1024]{1,0:T(8,128)}, u32[]{:S(2)}, u32[]{:S(2)}) collective-permute-start(f32[512,1024]{1,0:T(8,128)} %pad_maximum_fusion.12), channel_id=1, source_target_pairs={{0,1},{1,0},{2,3},{3,2},{4,5},{5,4},{6,7},{7,6}} | collective-permute-start | bytes 6291464 | tf_op jit(solution)/shard_map/ppermute | solution.py:227
  942.6 69.5 %collective-permute-start.22 = (f32[128,5120]{1,0:T(8,128)S(1)}, f32[128,5120]{1,0:T(8,128)}, u32[]{:S(2)}, u32[]{:S(2)}) collective-permute-start(f32[128,5120]{1,0:T(8,128)S(1)} %copy-done.4), channel_id=1, source_target_pairs={{0,1},{1,0},{2,3},{3,2},{4,5},{5,4},{6,7},{7,6}} | collective-permute-start | bytes 7864328 | tf_op jit(solution)/shard_map/ppermute | solution.py:96
  950.5 79.2 %collective-permute-start.23 = (f32[128,5120]{1,0:T(8,128)}, f32[128,5120]{1,0:T(8,128)}, u32[]{:S(2)}, u32[]{:S(2)}) collective-permute-start(f32[128,5120]{1,0:T(8,128)} %collective-permute-done.8.rest_2_), channel_id=1, source_target_pairs={{0,1},{1,0},{2,3},{3,2},{4,5},{5,4},{6,7},{7,6}} | collective-permute-start | bytes 7864328 | tf_op jit(solution)/shard_map/ppermute | solution.py:96
  950.7 79.0 %collective-permute-start.24 = (f32[128,5120]{1,0:T(8,128)}, f32[128,5120]{1,0:T(8,128)}, u32[]{:S(2)}, u32[]{:S(2)}) collective-permute-start(f32[128,5120]{1,0:T(8,128)} %collective-permute-done.9.rest_4_), channel_id=1, source_target_pairs={{0,1},{1,0},{2,3},{3,2},{4,5},{5,4},{6,7},{7,6}} | collective-permute-start | bytes 7864328 | tf_op jit(solution)/shard_map/ppermute | solution.py:96
  999.0 51.0 %collective-permute-start.25 = (f32[128,5120]{1,0:T(8,128)}, f32[128,5120]{1,0:T(8,128)}, u32[]{:S(2)}, u32[]{:S(2)}) collective-permute-start(f32[128,5120]{1,0:T(8,128)} %collective-permute-done.11.rest_6_), channel_id=1, source_target_pairs={{0,1},{1,0},{2,3},{3,2},{4,5},{5,4},{6,7},{7,6}} | collective-permute-start | bytes 7864328 | tf_op jit(solution)/shard_map/ppermute | solution.py:96
  1003.2 44.1 %collective-permute-start.13 = (f32[512,1024]{1,0:T(8,128)}, f32[512,1024]{1,0:T(8,128)}, u32[]{:S(2)}, u32[]{:S(2)}) collective-permute-start(f32[512,1024]{1,0:T(8,128)} %pad_maximum_fusion.11), channel_id=1, source_target_pairs={{0,1},{1,0},{2,3},{3,2},{4,5},{5,4},{6,7},{7,6}} | collective-permute-start | bytes 6291464 | tf_op jit(solution)/shard_map/ppermute | solution.py:227
  1012.2 38.4 %collective-permute-start.14 = (f32[128,2560]{1,0:T(8,128)}, f32[128,2560]{1,0:T(8,128)S(1)}, u32[]{:S(2)}, u32[]{:S(2)}) collective-permute-start(f32[128,2560]{1,0:T(8,128)} %copy-done.14), channel_id=1, source_target_pairs={{0,1},{1,0},{2,3},{3,2},{4,5},{5,4},{6,7},{7,6}} | collective-permute-start | bytes 3932168 | tf_op jit(solution)/shard_map/ppermute | solution.py:96
  1029.7 36.1 %collective-permute-start.16 = (f32[128,2560]{1,0:T(8,128)S(1)}, f32[128,2560]{1,0:T(8,128)}, u32[]{:S(2)}, u32[]{:S(2)}) collective-permute-start(f32[128,2560]{1,0:T(8,128)S(1)} %copy-done.15), channel_id=1, source_target_pairs={{0,4},{4,0},{1,5},{5,1},{2,6},{6,2},{3,7},{7,3}} | collective-permute-start | bytes 3932168 | tf_op jit(solution)/shard_map/ppermute | solution.py:95
  1029.8 82.7 %collective-permute-start.33 = (f32[256,2048]{1,0:T(8,128)S(1)}, f32[256,2048]{1,0:T(8,128)S(1)}, u32[]{:S(2)}, u32[]{:S(2)}) collective-permute-start(f32[256,2048]{1,0:T(8,128)S(1)} %fusion.50), channel_id=1, source_target_pairs={{0,2},{2,0},{1,3},{3,1},{4,6},{6,4},{5,7},{7,5}} | collective-permute-start | bytes 6291464 | tf_op jit(solution)/shard_map/ppermute | solution.py:222
  1047.3 19.0 %collective-permute-start.15 = (f32[128,2560]{1,0:T(8,128)S(1)}, f32[128,2560]{1,0:T(8,128)S(1)}, u32[]{:S(2)}, u32[]{:S(2)}) collective-permute-start(f32[128,2560]{1,0:T(8,128)S(1)} %copy-done.34), channel_id=1, source_target_pairs={{0,1},{1,0},{2,3},{3,2},{4,5},{5,4},{6,7},{7,6}} | collective-permute-start | bytes 3932168 | tf_op jit(solution)/shard_map/ppermute | solution.py:96
  1050.1 62.4 %collective-permute-start.27 = (f32[128,3072]{1,0:T(8,128)S(1)}, f32[128,3072]{1,0:T(8,128)S(1)}, u32[]{:S(2)}, u32[]{:S(2)}) collective-permute-start(f32[128,3072]{1,0:T(8,128)S(1)} %copy-done.10), channel_id=1, source_target_pairs={{0,2},{2,0},{1,3},{3,1},{4,6},{6,4},{5,7},{7,5}} | collective-permute-start | bytes 4718600 | tf_op jit(solution)/shard_map/ppermute | solution.py:93
  1050.5 63.6 %copy-start.35 = (f32[128,2560]{1,0:T(8,128)}, f32[128,2560]{1,0:T(8,128)S(1)}, u32[]{:S(2)}) copy-start(f32[128,2560]{1,0:T(8,128)S(1)} %collective-permute-done.14.rest_1_) | copy-start | bytes 3932164
  1050.5 133.5 %collective-permute-start.29 = (f32[1024,1024]{1,0:T(8,128)}, f32[1024,1024]{1,0:T(8,128)}, u32[]{:S(2)}, u32[]{:S(2)}) collective-permute-start(f32[1024,1024]{1,0:T(8,128)} %fusion.142.share_ref), channel_id=1, source_target_pairs={{0,1},{1,0},{2,3},{3,2},{4,5},{5,4},{6,7},{7,6}} | collective-permute-start | bytes 12582920 | tf_op jit(solution)/shard_map/ppermute | solution.py:232
  1065.8 54.1 %copy-start = (f32[1,1024,1024]{2,1,0:T(8,128)S(1)}, f32[1,1024,1024]{2,1,0:T(8,128)}, u32[]{:S(2)}) copy-start(f32[1,1024,1024]{2,1,0:T(8,128)} %get-tuple-element.68) | copy-start | bytes 12582916
  1065.8 54.1 %copy-start.1 = (f32[1,1024,1024]{2,1,0:T(8,128)S(1)}, f32[1,1024,1024]{2,1,0:T(8,128)}, u32[]{:S(2)}) copy-start(f32[1,1024,1024]{2,1,0:T(8,128)} %get-tuple-element.70) | copy-start | bytes 12582916
  1065.8 133.3 %collective-permute-start.30 = (f32[1024,1024]{1,0:T(8,128)}, f32[1024,1024]{1,0:T(8,128)}, u32[]{:S(2)}, u32[]{:S(2)}) collective-permute-start(f32[1024,1024]{1,0:T(8,128)} %fusion.134.share_ref), channel_id=1, source_target_pairs={{0,1},{1,0},{2,3},{3,2},{4,5},{5,4},{6,7},{7,6}} | collective-permute-start | bytes 12582920 | tf_op jit(solution)/shard_map/ppermute | solution.py:232
  1066.3 53.0 %copy-start.36 = (f32[128,2560]{1,0:T(8,128)}, f32[128,2560]{1,0:T(8,128)S(1)}, u32[]{:S(2)}) copy-start(f32[128,2560]{1,0:T(8,128)S(1)} %collective-permute-done.15.rest_3_) | copy-start | bytes 3932164
  1066.3 50.4 %collective-permute-start.18 = (f32[128,2560]{1,0:T(8,128)S(1)}, f32[128,2560]{1,0:T(8,128)}, u32[]{:S(2)}, u32[]{:S(2)}) collective-permute-start(f32[128,2560]{1,0:T(8,128)S(1)} %copy-done.34), channel_id=1, source_target_pairs={{0,4},{4,0},{1,5},{5,1},{2,6},{6,2},{3,7},{7,3}} | collective-permute-start | bytes 3932168 | tf_op jit(solution)/shard_map/ppermute | solution.py:95
  1112.4 4.4 collective-permute-start.26
  1112.5 5.6 collective-permute-start.28
  1116.7 78.2 %collective-permute-start.34 = (f32[512,1024]{1,0:T(8,128)}, f32[512,1024]{1,0:T(8,128)}, u32[]{:S(2)}, u32[]{:S(2)}) collective-permute-start(f32[512,1024]{1,0:T(8,128)} %pad_maximum_fusion.14), channel_id=1, source_target_pairs={{0,1},{1,0},{2,3},{3,2},{4,5},{5,4},{6,7},{7,6}} | collective-permute-start | bytes 6291464 | tf_op jit(solution)/shard_map/ppermute | solution.py:227
  1116.8 42.7 %collective-permute-start.17 = (f32[128,2560]{1,0:T(8,128)}, f32[128,2560]{1,0:T(8,128)S(1)}, u32[]{:S(2)}, u32[]{:S(2)}) collective-permute-start(f32[128,2560]{1,0:T(8,128)} %collective-permute-done.16.rest_4_), channel_id=1, source_target_pairs={{0,1},{1,0},{2,3},{3,2},{4,5},{5,4},{6,7},{7,6}} | collective-permute-start | bytes 3932168 | tf_op jit(solution)/shard_map/ppermute | solution.py:96
  1118.1 41.4 %collective-permute-start.19 = (f32[128,2560]{1,0:T(8,128)}, f32[128,2560]{1,0:T(8,128)}, u32[]{:S(2)}, u32[]{:S(2)}) collective-permute-start(f32[128,2560]{1,0:T(8,128)} %collective-permute-done.18.rest_6_), channel_id=1, source_target_pairs={{0,1},{1,0},{2,3},{3,2},{4,5},{5,4},{6,7},{7,6}} | collective-permute-start | bytes 3932168 | tf_op jit(solution)/shard_map/ppermute | solution.py:96
  1243.9 146.2 %collective-permute-start.38 = (f32[1024,1024]{1,0:T(8,128)}, f32[1024,1024]{1,0:T(8,128)}, u32[]{:S(2)}, u32[]{:S(2)}) collective-permute-start(f32[1024,1024]{1,0:T(8,128)} %fusion.150.share_ref), channel_id=1, source_target_pairs={{0,1},{1,0},{2,3},{3,2},{4,5},{5,4},{6,7},{7,6}} | collective-permute-start | bytes 12582920 | tf_op jit(solution)/shard_map/ppermute | solution.py:232
  1244.3 113.0 %collective-permute-start.31 = (f32[256,2048]{1,0:T(8,128)}, f32[256,2048]{1,0:T(8,128)}, u32[]{:S(2)}, u32[]{:S(2)}) collective-permute-start(f32[256,2048]{1,0:T(8,128)} %fusion.48), channel_id=1, source_target_pairs={{0,2},{2,0},{1,3},{3,1},{4,6},{6,4},{5,7},{7,5}} | collective-permute-start | bytes 6291464 | tf_op jit(solution)/shard_map/ppermute | solution.py:222
  1247.3 166.5 %copy-start.2 = (f32[128,3072]{1,0:T(8,128)}, f32[128,3072]{1,0:T(8,128)S(1)}, u32[]{:S(2)}) copy-start(f32[128,3072]{1,0:T(8,128)S(1)} %pad_maximum_fusion.15.rest_0_) | copy-start | bytes 4718596
  1247.4 106.7 %collective-permute-start.36 = (f32[128,3072]{1,0:T(8,128)S(1)}, f32[128,3072]{1,0:T(8,128)S(1)}, u32[]{:S(2)}, u32[]{:S(2)}) collective-permute-start(f32[128,3072]{1,0:T(8,128)S(1)} %pad_maximum_fusion.15.rest_0_), channel_id=1, source_target_pairs={{0,2},{2,0},{1,3},{3,1},{4,6},{6,4},{5,7},{7,5}} | collective-permute-start | bytes 4718600 | tf_op jit(solution)/shard_map/ppermute | solution.py:93
  1250.4 103.7 %collective-permute-start.40 = (f32[128,2560]{1,0:T(8,128)}, f32[128,2560]{1,0:T(8,128)}, u32[]{:S(2)}, u32[]{:S(2)}) collective-permute-start(f32[128,2560]{1,0:T(8,128)} %slice.149.rest_0_), channel_id=1, source_target_pairs={{0,2},{2,0},{1,3},{3,1},{4,6},{6,4},{5,7},{7,5}} | collective-permute-start | bytes 3932168 | tf_op jit(solution)/shard_map/ppermute | solution.py:93
  1251.9 111.4 %collective-permute-start.42 = (f32[128,2560]{1,0:T(8,128)}, f32[128,2560]{1,0:T(8,128)}, u32[]{:S(2)}, u32[]{:S(2)}) collective-permute-start(f32[128,2560]{1,0:T(8,128)} %slice.149.rest_0_), channel_id=1, source_target_pairs={{0,4},{4,0},{1,5},{5,1},{2,6},{6,2},{3,7},{7,3}} | collective-permute-start | bytes 3932168 | tf_op jit(solution)/shard_map/ppermute | solution.py:95
  1354.1 9.5 collective-permute-start.35
  1354.1 59.8 %copy-start.7 = (f32[128,3072]{1,0:T(8,128)}, f32[128,3072]{1,0:T(8,128)S(1)}, u32[]{:S(2)}) copy-start(f32[128,3072]{1,0:T(8,128)S(1)} %collective-permute-done.36.rest_2_) | copy-start | bytes 4718596
  1354.1 34.8 %collective-permute-start.37 = (f32[128,3072]{1,0:T(8,128)S(1)}, f32[128,3072]{1,0:T(8,128)S(1)}, u32[]{:S(2)}, u32[]{:S(2)}) collective-permute-start(f32[128,3072]{1,0:T(8,128)S(1)} %collective-permute-done.36.rest_2_), channel_id=1, source_target_pairs={{0,1},{1,0},{2,3},{3,2},{4,5},{5,4},{6,7},{7,6}} | collective-permute-start | bytes 4718600 | tf_op jit(solution)/shard_map/ppermute | solution.py:96
  1357.3 31.6 %collective-permute-start.44 = (f32[128,2560]{1,0:T(8,128)}, f32[128,2560]{1,0:T(8,128)}, u32[]{:S(2)}, u32[]{:S(2)}) collective-permute-start(f32[128,2560]{1,0:T(8,128)} %collective-permute-done.40.rest_2_), channel_id=1, source_target_pairs={{0,4},{4,0},{1,5},{5,1},{2,6},{6,2},{3,7},{7,3}} | collective-permute-start | bytes 3932168 | tf_op jit(solution)/shard_map/ppermute | solution.py:95
  1363.2 73.9 %collective-permute-start.32 = (f32[512,1024]{1,0:T(8,128)}, f32[512,1024]{1,0:T(8,128)}, u32[]{:S(2)}, u32[]{:S(2)}) collective-permute-start(f32[512,1024]{1,0:T(8,128)} %pad_maximum_fusion.13), channel_id=1, source_target_pairs={{0,1},{1,0},{2,3},{3,2},{4,5},{5,4},{6,7},{7,6}} | collective-permute-start | bytes 6291464 | tf_op jit(solution)/shard_map/ppermute | solution.py:227
  1363.5 77.8 %collective-permute-start.39 = (f32[128,2560]{1,0:T(8,128)}, f32[128,2560]{1,0:T(8,128)}, u32[]{:S(2)}, u32[]{:S(2)}) collective-permute-start(f32[128,2560]{1,0:T(8,128)} %slice.149.rest_0_), channel_id=1, source_target_pairs={{0,1},{1,0},{2,3},{3,2},{4,5},{5,4},{6,7},{7,6}} | collective-permute-start | bytes 3932168 | tf_op jit(solution)/shard_map/ppermute | solution.py:96
  1388.9 52.5 %collective-permute-start.41 = (f32[128,2560]{1,0:T(8,128)}, f32[128,2560]{1,0:T(8,128)}, u32[]{:S(2)}, u32[]{:S(2)}) collective-permute-start(f32[128,2560]{1,0:T(8,128)} %collective-permute-done.40.rest_2_), channel_id=1, source_target_pairs={{0,1},{1,0},{2,3},{3,2},{4,5},{5,4},{6,7},{7,6}} | collective-permute-start | bytes 3932168 | tf_op jit(solution)/shard_map/ppermute | solution.py:96
  1388.9 52.5 %collective-permute-start.43 = (f32[128,2560]{1,0:T(8,128)}, f32[128,2560]{1,0:T(8,128)}, u32[]{:S(2)}, u32[]{:S(2)}) collective-permute-start(f32[128,2560]{1,0:T(8,128)} %collective-permute-done.42.rest_4_), channel_id=1, source_target_pairs={{0,1},{1,0},{2,3},{3,2},{4,5},{5,4},{6,7},{7,6}} | collective-permute-start | bytes 3932168 | tf_op jit(solution)/shard_map/ppermute | solution.py:96
  1390.1 51.3 %collective-permute-start.45 = (f32[128,2560]{1,0:T(8,128)}, f32[128,2560]{1,0:T(8,128)}, u32[]{:S(2)}, u32[]{:S(2)}) collective-permute-start(f32[128,2560]{1,0:T(8,128)} %collective-permute-done.44.rest_6_), channel_id=1, source_target_pairs={{0,1},{1,0},{2,3},{3,2},{4,5},{5,4},{6,7},{7,6}} | collective-permute-start | bytes 3932168 | tf_op jit(solution)/shard_map/ppermute | solution.py:96
  1482.6 7.3 collective-permute-start.46
  (53 other events, 676.2 us)
Sparse Core Ops, SparseCore 0:
  80.7 81.6 reduce-scatter.8
  306.9 65.6 reduce-scatter.10
  431.5 106.9 reduce-scatter.12
  558.9 66.9 reduce-scatter.14
  628.2 53.3 reduce-scatter.20
  690.3 78.1 reduce-scatter.18
  804.1 94.3 reduce-scatter.16
  932.1 86.0 reduce-scatter.22
